TPU v7x, 256 devices: a whole 4x4x8 slice. The times are simulated.
256 devices in a mesh: gx: 8 (over y, core), gy: 8 (over z), gz: 4 (over x).
Axes of the slice: x: 4, y: 4, z: 8, core: 2. Of those that a mesh axis runs over, the one named last changes fastest.
Arguments:
- blocks: bfloat16 [1536, 64, 4096], P(('gx', 'gy', 'gz')), may hold values from -6 to 6
- ownership: int32 [1536, 3], P(('gx', 'gy', 'gz')), may hold values from -1 to 15, as said below
- basis_rows: bfloat16 [1024, 48], replicated, may hold values from -0.1875 to 0.1875
Outputs:
- gram_matrix: float32 [1024, 1024], P(('gx', 'gy', 'gz'))
Inputs may be any that keep to these rules, and one draw needn't show every extreme that they name: `ownership`: row d * 6 + s is slot s of device d in mesh order. Each row is a block triple (i, j, k) with i <= j <= k, or -1 -1 -1 for an empty slot; every such triple of blocks 0 to 15 stands in exactly one row; the live slots of a device come first; some device has all 6 slots live.
All inputs are finite; a program needn't handle non-finite values.
Results may differ from a plain program's by a relative error of at most 0.0037.
Values may be sent and summed in bfloat16 or wider, within the bound.
No kernel may reach another device: no remote copies, remote signals or barrier semaphores. Data moves between devices by JAX's collectives and lax.ppermute only.
A program may use at most 128 MiB of HBM per device.

v0:
```python
import jax
import jax.numpy as jnp
from jax import lax
from jax.sharding import Mesh
from jax.sharding import PartitionSpec as P

N = 1024
NB = 16
R = 48
GX_GY = ("gx_0", "gx_1", "gy")
GX_GY_GZ = ("gx_0", "gx_1", "gy", "gz")


ORDERS = ((0, 1, 2), (0, 2, 1), (1, 0, 2), (1, 2, 0), (2, 0, 1), (2, 1, 0))
REDUCE_FORMS = ("gxyz,gxq->gyzq", "gxyz,gyq->gxzq", "gxyz,gzq->gxyq")


def reduced_to_own(pieces, axes, turns):
    dims = [lax.axis_size(a) for a in axes]
    pieces = pieces.reshape(*dims, *pieces.shape[1:])
    pieces = pieces.transpose(*turns, *range(len(axes), pieces.ndim))
    pieces = pieces.reshape(-1, *pieces.shape[len(axes) :])
    for k in turns:
        pieces = lax.psum_scatter(pieces, axes[k], scatter_dimension=0, tiled=True)
    return pieces[0]


def in_blocks(shard, dim, devices):
    dims = shard.shape
    pieces = shard.reshape(*dims[:dim], devices, dims[dim] // devices, *dims[dim + 1 :])
    return jnp.moveaxis(pieces, dim, 0)


def scatter_axes(shard, axes, turns, dim):
    devices = lax.axis_size(axes)
    return reduced_to_own(in_blocks(shard, dim, devices), axes, turns)


def sent_and_summed(shard, axis, dim):
    pieces = in_blocks(shard, dim, lax.axis_size(axis))
    arrived = lax.all_to_all(pieces, axis, split_axis=0, concat_axis=0, tiled=True)
    return arrived.sum(axis=0)


def unpack(stored, unique_triples):
    number = stored.shape[0]
    extent = stored.shape[1]
    unpacked = stored.reshape(number, extent, extent, extent)
    leading_block_index = lax.broadcasted_iota(jnp.int32, (1, extent, extent, extent), 1)
    middle = lax.broadcasted_iota(jnp.int32, (1, extent, extent, extent), 2)
    trailing = lax.broadcasted_iota(jnp.int32, (1, extent, extent, extent), 3)
    same_front = (unique_triples[:, 0] == unique_triples[:, 1])[:, None, None, None]
    same_back = (unique_triples[:, 1] == unique_triples[:, 2])[:, None, None, None]

    def order_back(values):
        return jnp.where(middle <= trailing, values, jnp.swapaxes(values, 2, 3))

    unpacked = jnp.where(same_back, order_back(unpacked), unpacked)
    unpacked = jnp.where(
        same_front,
        jnp.where(leading_block_index <= middle, unpacked, jnp.swapaxes(unpacked, 1, 2)),
        unpacked,
    )
    unpacked = jnp.where(same_back, order_back(unpacked), unpacked)
    return unpacked


def slot_terms(stored, unique_triples, basis_rows):
    extent = stored.shape[1]
    columns = basis_rows.shape[1]
    unpacked = unpack(stored, unique_triples)
    basis_blocks = basis_rows.reshape(basis_rows.shape[0] // extent, extent, columns)
    selected_rows = jnp.take(
        basis_blocks, jnp.clip(unique_triples, 0, basis_blocks.shape[0] - 1), axis=0
    )
    factors = (selected_rows[:, 0], selected_rows[:, 1], selected_rows[:, 2])
    reduced = [
        jnp.einsum(
            REDUCE_FORMS[slot_pos], unpacked, factors[slot_pos], preferred_element_type=jnp.float32
        ).astype(jnp.bfloat16)
        for slot_pos in range(3)
    ]
    by_row = [0.0, 0.0, 0.0]
    for position in range(6):
        row_slot_index, middle_slot_index, last_slot = ORDERS[position]
        contraction_form = (
            "zixl,zxo->ziol" if row_slot_index < middle_slot_index else "hwie,hwy->hiye"
        )
        contrib = jnp.einsum(
            contraction_form,
            reduced[last_slot],
            factors[middle_slot_index],
            preferred_element_type=jnp.float32,
        )
        ordered = unique_triples[:, jnp.array(ORDERS[position])]
        distinct = unique_triples[:, 0] >= 0
        for earlier in ORDERS[:position]:
            distinct = distinct & jnp.any(ordered != unique_triples[:, jnp.array(earlier)], axis=1)
        by_row[row_slot_index] = by_row[row_slot_index] + jnp.where(
            distinct[:, None, None, None], contrib, 0.0
        )
    stacked = jnp.stack(by_row, axis=1)
    return stacked.reshape(stacked.shape[0], 3, extent, columns * columns)


def local(blocks, ownership, basis_rows):
    slot_total = blocks.shape[0]
    extent = N // NB
    pair_cols = R * R
    per_turn = min(8, slot_total)

    def add_group(batch_index, accumulated):
        first_slot = jnp.minimum(batch_index * per_turn, slot_total - per_turn)
        slot_locations = first_slot + jnp.arange(per_turn, dtype=jnp.int32)
        wanted = (slot_locations >= batch_index * per_turn) & (ownership[:, 0] >= 0)
        contribs = slot_terms(blocks, ownership, basis_rows)
        contribs = jnp.where(wanted[:, None, None, None], contribs, 0.0)
        targets = jnp.clip(ownership, 0, NB - 1).reshape(1, -1)
        onehot = (targets == jnp.arange(NB, dtype=jnp.int32)[:, None]).astype(jnp.float32)
        return accumulated + jnp.einsum(
            "nk,kbc->nbc",
            onehot,
            contribs.reshape(per_turn * 3, extent, pair_cols),
            precision=lax.Precision.HIGHEST,
        )

    zero_rows = jnp.zeros((NB, extent, pair_cols), jnp.float32)
    summed = lax.fori_loop(0, (slot_total + per_turn - 1) // per_turn, add_group, zero_rows)
    partial_value = summed.reshape(N, R, R)
    outgoing_rows = partial_value.reshape(N, pair_cols)
    first_section = scatter_axes(outgoing_rows, GX_GY, (1, 0, 2), 0)
    own_rows = sent_and_summed(first_section, "gz", 0)
    row_block = own_rows.reshape(-1, R, R)
    rounded = (
        (0.5 * (row_block + jnp.swapaxes(row_block, 1, 2)))
        .reshape(-1, pair_cols)
        .astype(jnp.bfloat16)
    )
    gram_rows = lax.dot_general(
        rounded,
        lax.all_gather(rounded, GX_GY_GZ, axis=0, tiled=True),
        (((1,), (1,)), ((), ())),
        preferred_element_type=jnp.float32,
    )
    return gram_rows / R


def solution(mesh):
    split = Mesh(
        mesh.devices.reshape(4, 2, mesh.shape["gy"], mesh.shape["gz"]), ("gx_0", "gx_1", "gy", "gz")
    )
    return jax.shard_map(
        local,
        mesh=split,
        in_specs=(P(GX_GY_GZ, None, None), P(GX_GY_GZ, None), P()),
        out_specs=P(GX_GY_GZ, None),
        check_vma=False,
    )
```

profile of v0, /device:TPU:1, one launch (start us, length us, event | category | flops | bytes accessed | tf_op | source)
XLA Modules:
  0.0 520.9 jit_solution(523102884144031336)
XLA Ops:
  9.0 9.7 %reshape.141 = bf16[6,64,64,64]{3,2,1,0:T(8,128)(2,1)} reshape(bf16[6,64,4096]{2,1,0:T(8,128)(2,1)} %param.23) | data formatting | bytes 6291456 | tf_op jit(solution)/shard_map/while/body/eval_jaxpr/reshape | solution.py:48
  18.7 9.5 %copy.118 = bf16[6,64,64,64]{2,1,3,0:T(8,128)(2,1)} copy(bf16[6,64,64,64]{3,2,1,0:T(8,128)(2,1)} %reshape.141) | data formatting | bytes 6291456 | tf_op jit(solution)/shard_map/while/body/eval_jaxpr/reshape | solution.py:48
  28.2 13.5 %select_select_fusion.2 = bf16[6,64,64,64]{3,1,2,0:T(8,128)(2,1)} fusion(bf16[6,64,64,64]{2,1,3,0:T(8,128)(2,1)} %copy.118, bf16[6,64,64,64]{3,2,1,0:T(8,128)(2,1)} %reshape.141, pred[6]{0:T(512)(128)(4,1)S(1)} %get-tuple-element.73, pred[64,64,64]{2,0,1:T(8,128)(4,1)S(1)} %iota_compare_fusion.1), kind=kLoop, calls=%fused_computation.13 | loop fusion | flops 3145728 | bytes 9699334 | tf_op jit(solution)/shard_map/while/body/eval_jaxpr/jit(_where)/select_n | solution.py:58
  41.7 11.8 %select_select_fusion.1 = bf16[6,64,64,64]{3,1,2,0:T(8,128)(2,1)} fusion(bf16[6,64,64,64]{3,1,2,0:T(8,128)(2,1)} %select_select_fusion.2, pred[6]{0:T(512)(128)(4,1)S(1)} %get-tuple-element.74, pred[64,64,64]{2,0,1:T(8,128)(4,1)S(1)} %iota_compare_fusion), kind=kLoop, calls=%fused_computation.12 | loop fusion | flops 3145728 | bytes 6553606 | tf_op jit(solution)/shard_map/while/body/eval_jaxpr/jit(_where)/select_n | solution.py:59
  53.5 11.9 %copy.122 = bf16[6,64,64,64]{2,1,3,0:T(8,128)(2,1)} copy(bf16[6,64,64,64]{3,1,2,0:T(8,128)(2,1)} %select_select_fusion.1) | data formatting | bytes 6291456 | tf_op jit(solution)/shard_map/while/body/eval_jaxpr/jit(_where)/select_n | solution.py:59
  65.4 15.1 %select_select_fusion = bf16[6,64,64,64]{3,1,2,0:T(8,128)(2,1)} fusion(bf16[6,64,64,64]{2,1,3,0:T(8,128)(2,1)} %copy.122, pred[6]{0:T(512)(128)(4,1)S(1)} %get-tuple-element.73, pred[64,64,64]{2,0,1:T(8,128)(4,1)S(1)} %iota_compare_fusion.1, bf16[6,64,64,64]{3,1,2,0:T(8,128)(2,1)} %select_select_fusion.2, pred[64,64,64]{2,0,1:T(8,128)(4,1)S(1)} %iota_compare_fusion, ...), kind=kLoop, calls=%fused_computation.11 | loop fusion | flops 6291456 | bytes 9961484 | tf_op jit(solution)/shard_map/while/body/eval_jaxpr/jit(_where)/select_n | solution.py:64
  97.6 7.3 %fusion.8 = f32[6,48,64,48]{2,1,3,0:T(8,128)} fusion(bf16[6,64,64,48]{2,3,1,0:T(8,128)(2,1)S(1)} %convolution_convert_fusion, bf16[6,3,64,48]{2,3,0,1:T(8,128)(2,1)S(1)} %copy_select_fusion), kind=kOutput, calls=%fused_computation.23 | convolution fusion | flops 113246208 | bytes 8331264 | tf_op jit(solution)/shard_map/while/body/eval_jaxpr/zixl,zxo->ziol/dot_general | solution.py:89
  105.0 8.4 %fusion.18 = bf16[6,64,64,48]{2,3,1,0:T(8,128)(2,1)} fusion(bf16[6,64,64,64]{3,1,2,0:T(8,128)(2,1)S(1)} %bitcast.82, bf16[6,3,64,48]{2,3,0,1:T(8,128)(2,1)S(1)} %copy_select_fusion), kind=kOutput, calls=%fused_computation.33 | convolution fusion | flops 152174592 | bytes 8724480 | tf_op jit(solution)/shard_map/while/body/eval_jaxpr/gxyz,gzq->gxyq/dot_general | solution.py:78
  116.9 9.9 %fusion.12 = f32[6,48,64,48]{2,1,3,0:T(8,128)} fusion(bf16[6,64,64,48]{2,3,1,0:T(8,128)(2,1)} %fusion.21, bf16[6,3,64,48]{2,3,0,1:T(8,128)(2,1)S(1)} %copy_select_fusion), kind=kOutput, calls=%fused_computation.27 | convolution fusion | flops 113246208 | bytes 5971968 | tf_op jit(solution)/shard_map/while/body/eval_jaxpr/zixl,zxo->ziol/dot_general | solution.py:89
  132.2 9.9 %copy.133 = f32[6,64,48,48]{3,2,1,0:T(8,128)} copy(f32[6,64,48,48]{1,2,3,0:T(8,128)} %add_bitcast_fusion) | data formatting | bytes 7077888 | tf_op jit(solution)/shard_map/while/body/eval_jaxpr/add | solution.py:99
  149.3 9.1 %add_bitcast_fusion.1 = f32[6,64,48,48]{1,2,3,0:T(8,128)} fusion(f32[6,48,64,48]{2,1,3,0:T(8,128)} %fusion.8, pred[6]{0:T(512)(128)(4,1)} %get-tuple-element.77, pred[6]{0:T(512)(128)(4,1)S(1)} %get-tuple-element.76, bf16[6,64,64,48]{2,3,1,0:T(8,128)(2,1)} %fusion.18, bf16[6,3,64,48]{2,3,0,1:T(8,128)(2,1)} %copy-done.2), kind=kOutput, calls=%fused_computation.15 | convolution fusion | flops 115900416 | bytes 15409670 | tf_op jit(solution)/shard_map/while/body/eval_jaxpr/hwie,hwy->hiye/dot_general | solution.py:89
  158.4 9.9 %copy.130 = f32[6,64,48,48]{3,2,1,0:T(8,128)} copy(f32[6,64,48,48]{1,2,3,0:T(8,128)} %add_bitcast_fusion.1) | data formatting | bytes 7077888 | tf_op jit(solution)/shard_map/while/body/eval_jaxpr/add | solution.py:99
  168.2 8.7 %stack.19 = f32[6,1,64,2304]{3,2,0,1:T(8,128)} reshape(f32[6,64,48,48]{3,2,1,0:T(8,128)} %copy.130) | data formatting | bytes 7077888 | tf_op jit(solution)/shard_map/while/body/eval_jaxpr/stack | solution.py:102
  176.9 11.8 %add_bitcast_fusion.2 = f32[6,64,48,48]{1,2,3,0:T(8,128)} fusion(f32[6,48,64,48]{2,1,3,0:T(8,128)} %fusion.12, pred[6]{0:T(512)(128)(4,1)S(1)} %get-tuple-element.75, pred[6]{0:T(512)(128)(4,1)S(1)} %get-tuple-element.72, bf16[6,64,64,48]{2,3,1,0:T(8,128)(2,1)} %fusion.18, bf16[6,3,64,48]{2,3,0,1:T(8,128)(2,1)} %copy-done.2), kind=kOutput, calls=%fused_computation.16 | convolution fusion | flops 115900416 | bytes 15409164 | tf_op jit(solution)/shard_map/while/body/eval_jaxpr/zixl,zxo->ziol/dot_general | solution.py:89
  188.7 9.9 %copy.127 = f32[6,64,48,48]{3,2,1,0:T(8,128)} copy(f32[6,64,48,48]{1,2,3,0:T(8,128)} %add_bitcast_fusion.2) | data formatting | bytes 7077888 | tf_op jit(solution)/shard_map/while/body/eval_jaxpr/add | solution.py:99
  198.6 8.5 %stack.18 = f32[6,1,64,2304]{3,2,0,1:T(8,128)} reshape(f32[6,64,48,48]{3,2,1,0:T(8,128)} %copy.127) | data formatting | bytes 7077888 | tf_op jit(solution)/shard_map/while/body/eval_jaxpr/stack | solution.py:102
  221.6 14.6 %fusion = f32[16,64,2304]{2,0,1:T(8,128)} fusion(f32[18,64,2304]{2,1,0:T(8,128)S(1)} %bitcast_select_fusion, s32[18]{0:T(128)S(1)} %eq.44), kind=kOutput, calls=%fused_computation.7 | convolution fusion | flops 509608224 | bytes 20054088 | tf_op jit(solution)/shard_map/while/body/eval_jaxpr/nk,kbc->nbc/dot_general | solution.py:120
  236.2 9.1 %copy.136 = f32[16,64,2304]{2,1,0:T(8,128)S(1)} copy(f32[16,64,2304]{2,0,1:T(8,128)} %fusion) | data formatting | bytes 18874368 | tf_op jit(solution)/shard_map/while/body/eval_jaxpr/nk,kbc->nbc/dot_general | solution.py:120
  250.0 27.1 %reduce-scatter.4.cloned.1.call-done = f32[32,16,2304]{2,1,0:T(8,128)} async-done(((f32[64,16,2304]{2,1,0:T(8,128)}), f32[32,16,2304]{2,1,0:T(8,128)}) %reduce-scatter.4.cloned.1.call-update) | async-done | bytes 4718608 | tf_op jit(solution)/shard_map/reduce_scatter | solution.py:24
  277.2 56.9 %reduce-scatter.6.cloned.1.call-done = f32[8,16,2304]{2,1,0:T(8,128)} async-done(((f32[32,16,2304]{2,1,0:T(8,128)}), f32[8,16,2304]{2,1,0:T(8,128)}) %reduce-scatter.6.cloned.1.call-update) | async-done | bytes 1179664 | tf_op jit(solution)/shard_map/reduce_scatter | solution.py:24
  334.2 37.1 %reduce-scatter.8.cloned.1.call-done = f32[1,16,2304]{2,1,0:T(8,128)} async-done(((f32[8,16,2304]{2,1,0:T(8,128)}), f32[1,16,2304]{2,1,0:T(8,128)}) %reduce-scatter.8.cloned.1.call-update) | async-done | bytes 147472 | tf_op jit(solution)/shard_map/reduce_scatter | solution.py:24
  372.3 8.8 %all_to_all.5 = f32[4,4,2304]{2,1,0:T(4,128)S(1)} all-to-all(f32[4,4,2304]{2,1,0:T(4,128)S(1)} %reshape_squeeze.3), channel_id=1, replica_groups=mesh['gx_0'=4,'gx_1'=2,'gy'=8,'gz'=4] {'gz'}, dimensions={0} | all-to-all | bytes 294912 | tf_op jit(solution)/shard_map/all_to_all | solution.py:41
  382.2 118.9 %all-gather.3.cloned.1.call-done = bf16[256,4,2304]{2,1,0:T(4,128)(2,1)} async-done(((bf16[1,4,2304]{2,1,0:T(4,128)(2,1)}), bf16[256,4,2304]{2,1,0:T(4,128)(2,1)}) %all-gather.3.cloned.1.call-update) | async-done | bytes 4718608 | tf_op jit(solution)/shard_map/all_gather | solution.py:141
  501.1 8.4 %reshape.203 = bf16[1024,2304]{1,0:T(8,128)(2,1)} reshape(bf16[256,4,2304]{2,1,0:T(4,128)(2,1)} %all-gather.3.cloned.1.call-done) | data formatting | bytes 9437184
  (85 shorter events, 61.1 us)
Async XLA Ops:
  6.5 270.6 %reduce-scatter.4.cloned.1.call-start = ((), (), s32[]{:S(2)}) async-start(), calls=%async_computation.4 | async-start | bytes 14155776 | tf_op jit(solution)/shard_map/reduce_scatter | solution.py:24
  65.4 15.2 %copy-start.3 = (bf16[1024,48]{0,1:T(8,128)(2,1)S(1)}, bf16[1024,48]{0,1:T(8,128)(2,1)}, u32[]{:S(2)}) copy-start(bf16[1024,48]{0,1:T(8,128)(2,1)} %param.25) | copy-start | bytes 294916
  81.6 4.4 slice-start
  81.7 45.7 %copy-start.2 = (bf16[6,3,64,48]{2,3,0,1:T(8,128)(2,1)}, bf16[6,3,64,48]{2,3,0,1:T(8,128)(2,1)S(1)}, u32[]{:S(2)}) copy-start(bf16[6,3,64,48]{2,3,0,1:T(8,128)(2,1)S(1)} %copy_select_fusion) | copy-start | bytes 331780
  81.7 4.7 slice-start.1
  105.0 8.4 %copy-start.8 = (s32[3]{0:T(128)S(1)}, s32[3]{0:T(128)}, u32[]{:S(2)}) copy-start(s32[3]{0:T(128)} %constant.88) | copy-start | bytes 40
  105.0 8.4 %copy-start.1 = (s32[6,3]{0,1:T(4,128)S(1)}, s32[6,3]{0,1:T(4,128)}, u32[]{:S(2)}) copy-start(s32[6,3]{0,1:T(4,128)} %param.24) | copy-start | bytes 220
  105.0 9.6 %copy-start.7 = (s32[3]{0:T(128)S(1)}, s32[3]{0:T(128)}, u32[]{:S(2)}) copy-start(s32[3]{0:T(128)} %constant.91) | copy-start | bytes 40
  105.0 10.2 %copy-start.6 = (s32[3]{0:T(128)S(1)}, s32[3]{0:T(128)}, u32[]{:S(2)}) copy-start(s32[3]{0:T(128)} %constant.90) | copy-start | bytes 40
  105.0 10.7 %copy-start.5 = (s32[3]{0:T(128)S(1)}, s32[3]{0:T(128)}, u32[]{:S(2)}) copy-start(s32[3]{0:T(128)} %constant.89) | copy-start | bytes 40
  105.0 11.3 %copy-start.4 = (s32[3]{0:T(128)S(1)}, s32[3]{0:T(128)}, u32[]{:S(2)}) copy-start(s32[3]{0:T(128)} %constant.92) | copy-start | bytes 40
  113.4 14.0 %slice-start.2 = ((s8[4718592]{0:T(1024)(128)(4,1)}), s8[524288]{0:T(1024)(128)(4,1)S(1)}, s32[]{:S(2)}) async-start(s8[4718592]{0:T(1024)(128)(4,1)} %bitcast.83), calls=%async_computation.10 | async-start | bytes 1048576
  116.9 10.5 %slice-start.3 = ((s8[4718592]{0:T(1024)(128)(4,1)}), s8[4194304]{0:T(1024)(128)(4,1)S(1)}, s32[]{:S(2)}) async-start(s8[4718592]{0:T(1024)(128)(4,1)} %bitcast.83), calls=%async_computation.11 | async-start | bytes 8388608
  116.9 10.5 %copy-start = (f32[6,48,64,48]{2,1,3,0:T(8,128)S(1)}, f32[6,48,64,48]{2,1,3,0:T(8,128)}, u32[]{:S(2)}) copy-start(f32[6,48,64,48]{2,1,3,0:T(8,128)} %fusion.6) | copy-start | bytes 10616836
  250.0 84.1 %reduce-scatter.6.cloned.1.call-start = ((), (), s32[]{:S(2)}) async-start(), calls=%async_computation.5 | async-start | bytes 5898240 | tf_op jit(solution)/shard_map/reduce_scatter | solution.py:24
  277.1 94.2 %reduce-scatter.8.cloned.1.call-start = ((), (), s32[]{:S(2)}) async-start(), calls=%async_computation.6 | async-start | bytes 1327104 | tf_op jit(solution)/shard_map/reduce_scatter | solution.py:24
  334.1 167.0 %all-gather.3.cloned.1.call-start = ((), (), s32[]{:S(2)}) async-start(), calls=%async_computation.7 | async-start | bytes 4737024 | tf_op jit(solution)/shard_map/all_gather | solution.py:141
Sparse Core Ops, SparseCore 0:
  250.1 26.9 reduce-scatter.3
  279.6 54.4 reduce-scatter.5
  336.6 34.6 reduce-scatter.7
  382.2 118.8 all-gather.2
where the time goes:
time: 531 us; the launch traced here: 521 us
  waiting for transfers between devices  240 us (45%)
  local copies, waits for them, and re-layouts  119 us (22%)
  matrix products  85.9 us (16%)
  other arithmetic  52.9 us (10%)
  between operations  13.9 us (3%)
  blocking collectives  8.82 us (2%)
    reduce_scatter x3, waiting for transfers between devices, reduced_to_own(): pieces = lax.psum_scatter(pieces, axes[k], scatter_dimension=0, tiled=True)  121 us
    all_gather x1, waiting for transfers between devices, local(): lax.all_gather(rounded, GX_GY_GZ, axis=0, tiled=True)  119 us
    dot_general x6, matrix products, slot_terms(): jnp.einsum(contraction_form, reduced[last_slot], factors[middle_slot_inde...  47 us
    add x3, local copies, waits for them, and re-layouts, slot_terms(): by_row[row_slot_index]  29.6 us
    another operation x4, local copies, waits for them, and re-layouts, slot_terms(): stacked = jnp.stack(by_row, axis=1)  29.2 us
    select_n x2, other arithmetic, unpack(): unpacked = jnp.where(same_back, order_back(unpacked), unpacked)  28.6 us
    dot_general x3, matrix products, slot_terms(): jnp.einsum(REDUCE_FORMS[slot_pos], unpacked, factors[slot_pos], preferred...  20 us
    reshape x2, local copies, waits for them, and re-layouts, unpack(): unpacked = stored.reshape(number, extent, extent, extent)  19.2 us
  transfers between devices with their start and end apart: 4, of which 4 were waited for; matrix products, arithmetic and copies ran while one was open for 0% of the time, Pallas kernels for 0%

commit v1 on v0

v1 whole, which is shorter than its diff:
```python
import jax
import jax.numpy as jnp
from jax import lax
from jax.experimental import pallas as pl
from jax.experimental.pallas import tpu as pltpu
from jax.sharding import Mesh
from jax.sharding import PartitionSpec as P

NB = 16
R = 48
BS = 64
HALF = BS // 2
PAIRS = R // 2
BLK = 8
QB = R // BLK
TRI = QB * (QB + 1) // 2
ROWS = TRI * BLK
LANES = 2 * BS
STRIDE = 104
F32 = jnp.float32
BF16 = jnp.bfloat16

NN = (((1,), (0,)), ((), ()))
NT = (((1,), (1,)), ((), ()))
TN = (((0,), (0,)), ((), ()))


def dot(a, b, dims=NN):
    return lax.dot_general(a, b, dims, preferred_element_type=F32)


def local_kernel(
    own, core, stored, basis, keep, send, acc, bases, masked, swapped, wide, with_y, with_x
):
    slot = pl.program_id(0)

    def low(rows):
        return lax.broadcasted_iota(jnp.int32, (rows, LANES), 1) < BS

    def tile(i):
        return slice(i * LANES, (i + 1) * LANES)

    def paired(first, second):
        mask = low(first.shape[0])
        return (
            jnp.where(mask, first, pltpu.roll(second, BS, 1)),
            jnp.where(mask, pltpu.roll(first, BS, 1), second),
        )

    def row_of_each(row):
        return wide[pl.ds(row, HALF, stride=STRIDE), :]

    @pl.when(slot == 0)
    def _():
        acc[...] = jnp.zeros_like(acc)
        for j in range(NB // 2):
            columns = basis[:, tile(j)]
            bases[2 * j] = columns[:, :BS]
            bases[2 * j + 1] = columns[:, BS:]

    v0 = own[slot, 0]
    v1 = own[slot, 1]
    v2 = own[slot, 2]

    @pl.when(v0 >= 0)
    def _():
        u0 = bases[v0]
        u1 = bases[v1]
        u2 = bases[v2]
        zero = jnp.zeros_like(u0)

        def twice(u):
            return jnp.concatenate(
                [jnp.concatenate([u, zero], 1), jnp.concatenate([zero, u], 1)], 0
            )

        both0 = twice(u0)
        both2 = twice(u2)
        both02 = jnp.concatenate([both0, both2], 1)

        for c in range(HALF // 2):
            first = stored[0, :, tile(c)].astype(F32)
            second = stored[0, :, tile(c + HALF // 2)].astype(F32)
            for k, part in enumerate(paired(first, second)):
                wide[(2 * c + k) * STRIDE : (2 * c + k) * STRIDE + BS, :] = part

        front = v0 == v1
        back = v1 == v2

        @pl.when(front | back)
        def _():
            x = lax.broadcasted_iota(jnp.int32, (BS, LANES), 0)
            lane = lax.broadcasted_iota(jnp.int32, (BS, LANES), 1)
            z = lane & (BS - 1)
            y_high = jnp.where(lane < BS, 0, HALF)

            def scale(i, carry):
                y = y_high + i
                dxy = jnp.where(front, x - y, -1)
                dyz = jnp.where(back, y - z, -1)
                w = jnp.where(dxy == 0, 0.5, 1.0) * jnp.where(dyz == 0, 0.5, 1.0)
                w = jnp.where((dxy == 0) & (dyz == 0), 1.0 / 6.0, w)
                w = jnp.where((dxy > 0) | (dyz > 0), 0.0, w)
                rows = pl.ds(pl.multiple_of(i * STRIDE, 8), BS)
                wide[rows, :] = wide[rows, :] * w
                return carry

            lax.fori_loop(0, HALF, scale, 0)

        for i in range(HALF):
            masked[:, tile(i)] = wide[i * STRIDE : i * STRIDE + BS, :].astype(BF16)
        for i in range(HALF):
            upper, lower = paired(row_of_each(i), row_of_each(i + HALF))
            swapped[:HALF, tile(i)] = upper.astype(BF16)
            swapped[HALF:, tile(i)] = lower.astype(BF16)

        def spread(values, target, place):
            for i in range(HALF):
                wide[i * STRIDE : i * STRIDE + R, :] = values[:, tile(i)]
            for j in range(PAIRS):
                upper, lower = paired(row_of_each(2 * j), row_of_each(2 * j + 1))
                target[:HALF, tile(place(j))] = upper.astype(BF16)
                target[HALF:, tile(place(j))] = lower.astype(BF16)

        spread(dot(u1, swapped[...]), with_x, lambda j: j)
        spread(dot(u0, masked[...]), with_y, lambda j: 2 * j + 1)
        for i in range(HALF):
            block = masked[:, tile(i)]
            wide[i * STRIDE : i * STRIDE + 2 * R, :] = dot(
                both2, jnp.concatenate([block, block], 0), NT
            )
        for j in range(PAIRS):
            for k in range(2):
                part = jnp.where(
                    low(HALF), row_of_each(k * R + 2 * j), row_of_each(k * R + 2 * j + 1)
                )
                with_y[k * HALF : (k + 1) * HALF, tile(2 * j)] = part.astype(BF16)

        def add(block, j, value):
            q = j // 4
            start = BLK * (q * (q + 1) // 2)
            rows = BLK * (q + 1)
            at = (block, j % 4, slice(start, start + rows), slice(None))
            acc[at] = acc[at] + value[:rows]

        for j in range(PAIRS):
            over_y = dot(u1, with_y[:, 2 * j * LANES : (2 * j + 2) * LANES])
            pair_x = with_x[:, tile(j)]
            pair_y = with_y[:, 2 * j * LANES : (2 * j + 2) * LANES]
            over_x = dot(u0, pair_x)
            lanes_x = dot(both2, jnp.concatenate([pair_x, pair_x], 0), NT)
            lanes_y = dot(both02, jnp.concatenate([pair_y, pair_y], 0), NT)
            keep_low = low(R)
            add(v0, j, over_y[:, :LANES] + jnp.where(keep_low, lanes_x[:R], lanes_x[R:]))
            add(v1, j, jnp.where(keep_low, lanes_y[:R], lanes_y[R:]))
            add(v2, j, over_y[:, LANES:] + over_x)

    @pl.when(slot == pl.num_programs(0) - 1)
    def _():
        mine = core[0]

        def write(m, carry):
            block = 4 * (m // 2) + m % 2
            keep[m // 2, :, m % 2] = acc[block + 2 * mine]
            send[m // 2, :, m % 2] = acc[block + 2 * (1 - mine)].astype(BF16)
            return carry

        lax.fori_loop(0, NB // 2, write, 0)


def local_products(blocks, ownership, basis, core):
    slots = blocks.shape[0]
    half = (4, 4, 2, ROWS, LANES)
    whole = pl.BlockSpec(half, lambda s, own, core: (0, 0, 0, 0, 0))
    return pl.pallas_call(
        local_kernel,
        grid_spec=pltpu.PrefetchScalarGridSpec(
            num_scalar_prefetch=2,
            grid=(slots,),
            in_specs=[
                pl.BlockSpec((1, BS, BS * BS), lambda s, own, core: (s, 0, 0)),
                pl.BlockSpec(basis.shape, lambda s, own, core: (0, 0)),
            ],
            out_specs=[whole, whole],
            scratch_shapes=[
                pltpu.VMEM((NB, 4, ROWS, LANES), F32),
                pltpu.VMEM((NB, R, BS), BF16),
                pltpu.VMEM((BS, BS * BS), BF16),
                pltpu.VMEM((BS, BS * BS), BF16),
                pltpu.VMEM((HALF * STRIDE, LANES), F32),
                pltpu.VMEM((BS, 2 * PAIRS * LANES), BF16),
                pltpu.VMEM((BS, PAIRS * LANES), BF16),
            ],
        ),
        out_shape=[jax.ShapeDtypeStruct(half, F32), jax.ShapeDtypeStruct(half, BF16)],
        compiler_params=pltpu.CompilerParams(vmem_limit_bytes=56 << 20),
        name="local_products",
    )(ownership, core, blocks, basis)


def local(blocks, ownership, basis_rows):
    core = lax.axis_index("gx_1").astype(jnp.int32).reshape(1)
    kept, sent = local_products(blocks, ownership, basis_rows.T, core)
    arrived = lax.ppermute(sent, "gx_1", [(0, 1), (1, 0)])
    pair = (kept + arrived.astype(F32)).astype(BF16)
    pieces = lax.all_to_all(
        pair.reshape(16, 2 * ROWS, LANES), ("gx_0", "gz"), 0, 0, tiled=True
    )
    plane = pieces.astype(F32).sum(axis=0)
    plane = plane.reshape(2 * TRI, BLK, LANES).swapaxes(0, 1)
    pieces = lax.all_to_all(plane, "gy", 0, 0, tiled=True)
    rounded = pieces.sum(axis=0).astype(BF16)
    rounded = rounded.reshape(2, TRI, 2, BS).transpose(2, 1, 0, 3).reshape(2 * TRI, LANES)
    tri = [2.0 if p < q else 1.0 for q in range(QB) for p in range(q + 1)]
    weight = jnp.array(tri + tri, BF16)[:, None]
    copies = jnp.broadcast_to(rounded, (8, 2 * TRI, LANES))
    gathered = lax.all_to_all(copies, ("gx_0", "gx_1"), 0, 0, tiled=True)
    gram = dot(rounded * weight, gathered, (((0,), (1,)), ((), ())))
    gram = gram.reshape(32, 4, 8 * LANES)
    pieces = lax.all_to_all(gram, ("gy", "gz"), 0, 0, tiled=True)
    return pieces.sum(axis=0) / R


def solution(mesh):
    split = Mesh(
        mesh.devices.reshape(4, 2, mesh.shape["gy"], mesh.shape["gz"]), ("gx_0", "gx_1", "gy", "gz")
    )
    axes = ("gx_0", "gx_1", "gy", "gz")
    return jax.shard_map(
        local,
        mesh=split,
        in_specs=(P(axes, None, None), P(axes, None), P()),
        out_specs=P(axes, None),
        check_vma=False,
    )
```

time: 531 us -> 108 us (0.20); the launches traced: 521 us -> 106 us
  waiting for transfers between devices: 240 us -> 8.13 us
  local copies, waits for them, and re-layouts: 119 us -> 2.79 us
  matrix products: 85.9 us -> 0.2 us
  blocking collectives: 8.82 us -> 63.9 us
  other arithmetic: 52.9 us -> 3.08 us
  Pallas kernels: 0 us -> 21.7 us
  between operations: 13.9 us -> 0.07 us
  starting transfers between devices: 0.12 us -> 6.15 us
    reduce_scatter x3 -> x0, waiting for transfers between devices: 121 us -> none  [reduced_to_own(): pieces = lax.psum_scatter(pieces, axes[k], scatter_dimension=0, tiled=True)]
    all_gather x1 -> x0, waiting for transfers between devices: 119 us -> none  [local(): lax.all_gather(rounded, GX_GY_GZ, axis=0, tiled=True)]
    dot_general x11 -> x1, matrix products: 85.9 us -> 0.2 us  [dot(): return lax.dot_general(a, b, dims, preferred_element_type=F32)]
    all_to_all x1 -> x3, blocking collectives: 8.82 us -> 63.9 us  [the longest x1 28.3 us: local(): lax.all_to_all(pair.reshape(16, 2 * ROWS, LANES), ('gx_0', 'gz'), 0, 0, t...]
    select_n x5 -> x0, other arithmetic: 45.7 us -> none  [the longest x2 28.6 us: unpack(): unpacked = jnp.where(same_back, order_back(unpacked), unpacked)]
    another operation x6 -> x0, local copies, waits for them, and re-layouts: 30.2 us -> none  [the longest x4 29.2 us: slot_terms(): stacked = jnp.stack(by_row, axis=1)]
    add x3 -> x0, local copies, waits for them, and re-layouts: 29.6 us -> none  [slot_terms(): by_row[row_slot_index]]
    pallas_call x0 -> x1, Pallas kernels: none -> 21.7 us  [local_products(): pl.pallas_call(local_kernel, grid_spec=pltpu.PrefetchScalarGridSpec(num_s...]
  transfers between devices with their start and end apart: 4 -> 2, of which waited for: 4 -> 2; matrix products, arithmetic and copies ran while one was open for 0% -> 0% of each run, Pallas kernels for 0% -> 0%
where the time goes in v1:
time: 108 us; the launch traced here: 106 us
  blocking collectives  63.9 us (59%)
  Pallas kernels  21.7 us (20%)
  waiting for transfers between devices  8.13 us (8%)
  starting transfers between devices  6.15 us (6%)
  other arithmetic  3.08 us (3%)
  local copies, waits for them, and re-layouts  2.79 us (3%)
    all_to_all x1, blocking collectives, local(): lax.all_to_all(pair.reshape(16, 2 * ROWS, LANES), ('gx_0', 'gz'), 0, 0, t...  28.3 us
    pallas_call x1, Pallas kernels, local_products(): pl.pallas_call(local_kernel, grid_spec=pltpu.PrefetchScalarGridSpec(num_s...  21.7 us
    all_to_all x1, blocking collectives, local(): pieces = lax.all_to_all(gram, ('gy', 'gz'), 0, 0, tiled=True)  19.4 us
    all_to_all x1, blocking collectives, local(): pieces = lax.all_to_all(plane, 'gy', 0, 0, tiled=True)  16.3 us
    all_to_all x1, starting transfers between devices, local(): gathered = lax.all_to_all(copies, ('gx_0', 'gx_1'), 0, 0, tiled=True)  6.15 us
    all_to_all x1, waiting for transfers between devices, local(): gathered = lax.all_to_all(copies, ('gx_0', 'gx_1'), 0, 0, tiled=True)  4.8 us
    ppermute x1, waiting for transfers between devices, local(): arrived = lax.ppermute(sent, 'gx_1', [(0, 1), (1, 0)])  3.34 us
  transfers between devices with their start and end apart: 2, of which 2 were waited for; matrix products, arithmetic and copies ran while one was open for 0% of the time, Pallas kernels for 0%

profile of v1, /device:TPU:1, one launch (start us, length us, event | category | flops | bytes accessed | tf_op | source)
XLA Modules:
  0.0 106.1 jit_solution(6293421876633537816)
XLA Ops:
  0.0 1.4 %copy.19.own = s32[6,3]{1,0:T(8,128)} copy(s32[6,3]{0,1:T(4,128)} %param.5) | data formatting | bytes 144 | tf_op args[1]
  1.4 21.7 %local_products.1 = (f32[4,4,2,168,128]{4,3,2,1,0:T(8,128)}, bf16[4,4,2,168,128]{4,3,2,1,0:T(8,128)(2,1)}) custom-call(s32[6,3]{1,0:T(8,128)} %copy.19.own, s32[1]{0:T(128)} %bitcast.core, bf16[6,64,4096]{2,1,0:T(8,128)(2,1)} %stored.1, bf16[48,1024]{1,0:T(8,128)(2,1)} %bitcast.18), custom_call_target="tpu_custom_call" | custom-call | tf_op jit(solution)/shard_map/local_products/pallas_call | solution.py:175
  23.1 0.0 collective-permute-start
  23.1 3.3 %collective-permute-done = bf16[4,4,2,168,128]{4,3,2,1,0:T(8,128)(2,1)S(1)} collective-permute-done((bf16[4,4,2,168,128]{4,3,2,1,0:T(8,128)(2,1)}, bf16[4,4,2,168,128]{4,3,2,1,0:T(8,128)(2,1)S(1)}, u32[]{:S(2)}, u32[]{:S(2)}) %collective-permute-start) | collective-permute-done | bytes 1376288 | tf_op jit(solution)/shard_map/ppermute | solution.py:204
  26.4 2.1 %add_convert_fusion = bf16[4,4,2,168,128]{4,3,2,1,0:T(8,128)(2,1)S(1)} fusion(f32[4,4,2,168,128]{4,3,2,1,0:T(8,128)} %get-tuple-element.7, bf16[4,4,2,168,128]{4,3,2,1,0:T(8,128)(2,1)S(1)} %collective-permute-done), kind=kLoop, calls=%fused_computation.1 | loop fusion | flops 2064384 | bytes 5505024 | tf_op jit(solution)/shard_map/convert_element_type | solution.py:205
  28.5 28.3 %all_to_all.20 = bf16[16,336,128]{2,1,0:T(8,128)(2,1)S(1)} all-to-all(bf16[16,336,128]{2,1,0:T(8,128)(2,1)S(1)} %bitcast.14), channel_id=1, replica_groups=mesh['gx_0'=4,'gx_1'=2,'gy'=8,'gz'=4] {'gx_0','gz'}, dimensions={0} | all-to-all | bytes 2752512 | tf_op jit(solution)/shard_map/all_to_all | solution.py:206
  56.8 0.0 copy-start
  56.8 0.2 convert_reduce_fusion
  57.0 16.3 %all_to_all.21 = f32[8,42,128]{2,1,0:T(8,128)S(1)} all-to-all(f32[8,42,128]{2,1,0:T(8,128)S(1)} %copy.20), channel_id=1, replica_groups=mesh['gx_0'=4,'gx_1'=2,'gy'=8,'gz'=4] {'gy'}, dimensions={0} | all-to-all | bytes 344064 | tf_op jit(solution)/shard_map/all_to_all | solution.py:211
  73.3 0.1 convert_element_type.20
  73.4 0.1 reshape.22
  73.5 0.6 broadcast_in_dim.4
  74.2 6.2 %all-to-all-start.2 = ((bf16[8,42,128]{2,1,0:T(8,128)(2,1)}), bf16[8,42,128]{2,1,0:T(8,128)(2,1)S(1)}, u32[]{:S(2)}, u32[]{:S(2)}) async-start(bf16[8,42,128]{2,1,0:T(8,128)(2,1)} %broadcast_in_dim.4), calls=%async_computation.2 | async-start | bytes 196608 | tf_op jit(solution)/shard_map/all_to_all | solution.py:217
  80.3 0.0 copy-done
  80.3 0.1 multiply_bitcast_fusion
  80.4 0.1 copy.22
  80.5 4.8 %all-to-all-done.2 = bf16[8,42,128]{2,1,0:T(8,128)(2,1)S(1)} async-done(((bf16[8,42,128]{2,1,0:T(8,128)(2,1)}), bf16[8,42,128]{2,1,0:T(8,128)(2,1)S(1)}, u32[]{:S(2)}, u32[]{:S(2)}) %all-to-all-start.2) | async-done | bytes 86048 | tf_op jit(solution)/shard_map/all_to_all | solution.py:217
  85.3 0.1 reshape.23
  85.4 0.2 fusion
  85.6 0.3 copy.25
  86.0 19.4 %all_to_all.22 = f32[32,4,1024]{2,1,0:T(4,128)S(1)} all-to-all(f32[32,4,1024]{2,1,0:T(4,128)S(1)} %copy.25), channel_id=1, replica_groups=mesh['gx_0'=4,'gx_1'=2,'gy'=8,'gz'=4] {'gy','gz'}, dimensions={0} | all-to-all | bytes 1048576 | tf_op jit(solution)/shard_map/all_to_all | solution.py:220
  105.4 0.1 reduce_sum.29
  105.5 0.6 broadcast_multiply_fusion
  (4 shorter events, 0.1 us)
Async XLA Ops:
  23.1 3.3 %collective-permute-start = (bf16[4,4,2,168,128]{4,3,2,1,0:T(8,128)(2,1)}, bf16[4,4,2,168,128]{4,3,2,1,0:T(8,128)(2,1)S(1)}, u32[]{:S(2)}, u32[]{:S(2)}) collective-permute-start(bf16[4,4,2,168,128]{4,3,2,1,0:T(8,128)(2,1)} %get-tuple-element.8), channel_id=1, source_target_pairs={{0,32},{32,0},{1,33},{33,1},{2,34},{34,2},{3,35},{35,3},{4,36},{36... | collective-permute-start | bytes 4128776 | tf_op jit(solution)/shard_map/ppermute | solution.py:204
  56.8 23.5 %copy-start = (bf16[42]{0:T(256)(128)(2,1)S(1)}, bf16[42]{0:T(256)(128)(2,1)}, u32[]{:S(2)}) copy-start(bf16[42]{0:T(256)(128)(2,1)} %constant.13.clone) | copy-start | bytes 256
  74.2 11.2 %all-to-all-start.2 = ((bf16[8,42,128]{2,1,0:T(8,128)(2,1)}), bf16[8,42,128]{2,1,0:T(8,128)(2,1)S(1)}, u32[]{:S(2)}, u32[]{:S(2)}) async-start(bf16[8,42,128]{2,1,0:T(8,128)(2,1)} %broadcast_in_dim.4), calls=%async_computation.2 | async-start | bytes 196608 | tf_op jit(solution)/shard_map/all_to_all | solution.py:217

commit v2 on v1

--- a/solution.py
+++ b/solution.py
@@ -10,13 +10,14 @@
 R = 48
 BS = 64
 HALF = BS // 2
+QUARTER = BS // 4
 PAIRS = R // 2
 BLK = 8
 QB = R // BLK
 TRI = QB * (QB + 1) // 2
 ROWS = TRI * BLK
 LANES = 2 * BS
-STRIDE = 104
+STRIDE = 105
 F32 = jnp.float32
 BF16 = jnp.bfloat16
 
@@ -47,8 +48,8 @@
             jnp.where(mask, pltpu.roll(first, BS, 1), second),
         )
 
-    def row_of_each(row):
-        return wide[pl.ds(row, HALF, stride=STRIDE), :]
+    def row_of_each(row, count=HALF):
+        return wide[pl.ds(row, count, stride=STRIDE), :]
 
     @pl.when(slot == 0)
     def _():
@@ -58,9 +59,9 @@
             bases[2 * j] = columns[:, :BS]
             bases[2 * j + 1] = columns[:, BS:]
 
-    v0 = own[slot, 0]
-    v1 = own[slot, 1]
-    v2 = own[slot, 2]
+    v0 = own[0, slot]
+    v1 = own[1, slot]
+    v2 = own[2, slot]
 
     @pl.when(v0 >= 0)
     def _():
@@ -82,7 +83,9 @@
             first = stored[0, :, tile(c)].astype(F32)
             second = stored[0, :, tile(c + HALF // 2)].astype(F32)
             for k, part in enumerate(paired(first, second)):
-                wide[(2 * c + k) * STRIDE : (2 * c + k) * STRIDE + BS, :] = part
+                i = 2 * c + k
+                wide[i * STRIDE : i * STRIDE + BS, :] = part
+                masked[:, tile(i)] = part.astype(BF16)
 
         front = v0 == v1
         back = v1 == v2
@@ -101,14 +104,14 @@
                 w = jnp.where(dxy == 0, 0.5, 1.0) * jnp.where(dyz == 0, 0.5, 1.0)
                 w = jnp.where((dxy == 0) & (dyz == 0), 1.0 / 6.0, w)
                 w = jnp.where((dxy > 0) | (dyz > 0), 0.0, w)
-                rows = pl.ds(pl.multiple_of(i * STRIDE, 8), BS)
-                wide[rows, :] = wide[rows, :] * w
+                rows = pl.ds(i * STRIDE, BS)
+                scaled = wide[rows, :] * w
+                wide[rows, :] = scaled
+                masked[:, pl.ds(pl.multiple_of(i * LANES, LANES), LANES)] = scaled.astype(BF16)
                 return carry
 
-            lax.fori_loop(0, HALF, scale, 0)
-
-        for i in range(HALF):
-            masked[:, tile(i)] = wide[i * STRIDE : i * STRIDE + BS, :].astype(BF16)
+            lax.fori_loop(0, HALF, scale, 0, unroll=4)
+
         for i in range(HALF):
             upper, lower = paired(row_of_each(i), row_of_each(i + HALF))
             swapped[:HALF, tile(i)] = upper.astype(BF16)
@@ -124,17 +127,19 @@
 
         spread(dot(u1, swapped[...]), with_x, lambda j: j)
         spread(dot(u0, masked[...]), with_y, lambda j: 2 * j + 1)
-        for i in range(HALF):
-            block = masked[:, tile(i)]
+        for i in range(QUARTER):
+            both_tiles = [masked[:, tile(i)], masked[:, tile(i + QUARTER)]]
             wide[i * STRIDE : i * STRIDE + 2 * R, :] = dot(
-                both2, jnp.concatenate([block, block], 0), NT
+                both2, jnp.concatenate(both_tiles, 0), NT
             )
         for j in range(PAIRS):
             for k in range(2):
-                part = jnp.where(
-                    low(HALF), row_of_each(k * R + 2 * j), row_of_each(k * R + 2 * j + 1)
+                parts = paired(
+                    row_of_each(k * R + 2 * j, QUARTER), row_of_each(k * R + 2 * j + 1, QUARTER)
                 )
-                with_y[k * HALF : (k + 1) * HALF, tile(2 * j)] = part.astype(BF16)
+                for h in range(2):
+                    top = (2 * k + h) * QUARTER
+                    with_y[top : top + QUARTER, tile(2 * j)] = parts[h].astype(BF16)
 
         def add(block, j, value):
             q = j // 4
@@ -143,17 +148,33 @@
             at = (block, j % 4, slice(start, start + rows), slice(None))
             acc[at] = acc[at] + value[:rows]
 
-        for j in range(PAIRS):
-            over_y = dot(u1, with_y[:, 2 * j * LANES : (2 * j + 2) * LANES])
-            pair_x = with_x[:, tile(j)]
-            pair_y = with_y[:, 2 * j * LANES : (2 * j + 2) * LANES]
-            over_x = dot(u0, pair_x)
-            lanes_x = dot(both2, jnp.concatenate([pair_x, pair_x], 0), NT)
-            lanes_y = dot(both02, jnp.concatenate([pair_y, pair_y], 0), NT)
-            keep_low = low(R)
-            add(v0, j, over_y[:, :LANES] + jnp.where(keep_low, lanes_x[:R], lanes_x[R:]))
-            add(v1, j, jnp.where(keep_low, lanes_y[:R], lanes_y[R:]))
-            add(v2, j, over_y[:, LANES:] + over_x)
+        def stacked(ref, tiles):
+            return jnp.concatenate([ref[:, t] for t in tiles], 0)
+
+        for g in range(QB // 2):
+            rows = 2 * BLK * (g + 1)
+            tiles = range(8 * g, 8 * g + 8)
+            span_y = slice(16 * g * LANES, 16 * (g + 1) * LANES)
+            span_x = slice(8 * g * LANES, 8 * (g + 1) * LANES)
+            over_y = dot(u1[:rows], with_y[:, span_y])
+            over_x = dot(u0[:rows], with_x[:, span_x])
+            kept2 = jnp.concatenate([both2[:rows], both2[R : R + rows]], 0)
+            kept02 = jnp.concatenate([both02[:rows], both02[R : R + rows]], 0)
+            lanes_x = dot(kept2, stacked(with_x, [tile(j) for j in tiles]), NT)
+            lanes_y = dot(
+                kept02,
+                stacked(with_y, [slice(2 * j * LANES, (2 * j + 2) * LANES) for j in tiles]),
+                NT,
+            )
+            for k in range(4):
+                from_x = paired(lanes_x[:rows, tile(k)], lanes_x[rows:, tile(k)])
+                from_y = paired(lanes_y[:rows, tile(k)], lanes_y[rows:, tile(k)])
+                for h in range(2):
+                    i = 2 * k + h
+                    j = 8 * g + i
+                    add(v0, j, over_y[:, tile(2 * i)] + from_x[h])
+                    add(v1, j, from_y[h])
+                    add(v2, j, over_y[:, tile(2 * i + 1)] + over_x[:, tile(i)])
 
     @pl.when(slot == pl.num_programs(0) - 1)
     def _():
@@ -171,7 +192,6 @@
 def local_products(blocks, ownership, basis, core):
     slots = blocks.shape[0]
     half = (4, 4, 2, ROWS, LANES)
-    whole = pl.BlockSpec(half, lambda s, own, core: (0, 0, 0, 0, 0))
     return pl.pallas_call(
         local_kernel,
         grid_spec=pltpu.PrefetchScalarGridSpec(
@@ -181,7 +201,7 @@
                 pl.BlockSpec((1, BS, BS * BS), lambda s, own, core: (s, 0, 0)),
                 pl.BlockSpec(basis.shape, lambda s, own, core: (0, 0)),
             ],
-            out_specs=[whole, whole],
+            out_specs=[pl.BlockSpec(memory_space=pltpu.VMEM)] * 2,
             scratch_shapes=[
                 pltpu.VMEM((NB, 4, ROWS, LANES), F32),
                 pltpu.VMEM((NB, R, BS), BF16),
@@ -193,9 +213,41 @@
             ],
         ),
         out_shape=[jax.ShapeDtypeStruct(half, F32), jax.ShapeDtypeStruct(half, BF16)],
-        compiler_params=pltpu.CompilerParams(vmem_limit_bytes=56 << 20),
+        compiler_params=pltpu.CompilerParams(vmem_limit_bytes=48 << 20),
         name="local_products",
-    )(ownership, core, blocks, basis)
+    )(ownership.T, core, blocks, basis)
+
+
+def gram_kernel(mine, gathered, out):
+    depth = mine.shape[0]
+    low = lax.broadcasted_iota(jnp.int32, (depth, LANES), 1) < BS
+    pair = lax.broadcasted_iota(jnp.int32, (depth, LANES), 0) // 2
+    on_diagonal = pair < 0
+    for q in range(QB):
+        on_diagonal = on_diagonal | (pair == q * (q + 3) // 2)
+    weighted = (mine[...].astype(F32) * jnp.where(on_diagonal, 1.0, 2.0)).astype(BF16)
+    lows = []
+    highs = []
+    for g in range(0, NB, 2):
+        first = gathered[g].astype(F32)
+        second = gathered[g + 1].astype(F32)
+        lows.append(jnp.where(low, first, pltpu.roll(second, BS, 1)).astype(BF16))
+        highs.append(jnp.where(low, pltpu.roll(first, BS, 1), second).astype(BF16))
+    gram = dot(weighted[:, :BS], jnp.concatenate(lows, 1), TN)
+    gram = gram + dot(weighted[:, BS:], jnp.concatenate(highs, 1), TN)
+    for i in range(16):
+        out[i] = gram[4 * i : 4 * i + 4].astype(out.dtype)
+
+
+def gram_part(mine, gathered):
+    return pl.pallas_call(
+        gram_kernel,
+        in_specs=[pl.BlockSpec(memory_space=pltpu.VMEM)] * 2,
+        out_specs=pl.BlockSpec(memory_space=pltpu.VMEM),
+        out_shape=jax.ShapeDtypeStruct((16, 4, NB * BS), F32),
+        compiler_params=pltpu.CompilerParams(vmem_limit_bytes=16 << 20),
+        name="gram_part",
+    )(mine, gathered)
 
 
 def local(blocks, ownership, basis_rows):
@@ -207,25 +259,19 @@
         pair.reshape(16, 2 * ROWS, LANES), ("gx_0", "gz"), 0, 0, tiled=True
     )
     plane = pieces.astype(F32).sum(axis=0)
-    plane = plane.reshape(2 * TRI, BLK, LANES).swapaxes(0, 1)
-    pieces = lax.all_to_all(plane, "gy", 0, 0, tiled=True)
+    plane = plane.reshape(2, TRI, 4, 2, LANES).transpose(0, 2, 1, 3, 4)
+    plane = plane.reshape(8, 2 * TRI, LANES)
+    pieces = lax.all_to_all(plane, ("gy_0", "gy_1"), 0, 0, tiled=True)
     rounded = pieces.sum(axis=0).astype(BF16)
-    rounded = rounded.reshape(2, TRI, 2, BS).transpose(2, 1, 0, 3).reshape(2 * TRI, LANES)
-    tri = [2.0 if p < q else 1.0 for q in range(QB) for p in range(q + 1)]
-    weight = jnp.array(tri + tri, BF16)[:, None]
-    copies = jnp.broadcast_to(rounded, (8, 2 * TRI, LANES))
-    gathered = lax.all_to_all(copies, ("gx_0", "gx_1"), 0, 0, tiled=True)
-    gram = dot(rounded * weight, gathered, (((0,), (1,)), ((), ())))
-    gram = gram.reshape(32, 4, 8 * LANES)
-    pieces = lax.all_to_all(gram, ("gy", "gz"), 0, 0, tiled=True)
+    copies = jnp.broadcast_to(rounded, (16, 2 * TRI, LANES))
+    gathered = lax.all_to_all(copies, ("gx_0", "gx_1", "gy_0"), 0, 0, tiled=True)
+    pieces = lax.all_to_all(gram_part(rounded, gathered), ("gy_1", "gz"), 0, 0, tiled=True)
     return pieces.sum(axis=0) / R
 
 
 def solution(mesh):
-    split = Mesh(
-        mesh.devices.reshape(4, 2, mesh.shape["gy"], mesh.shape["gz"]), ("gx_0", "gx_1", "gy", "gz")
-    )
-    axes = ("gx_0", "gx_1", "gy", "gz")
+    axes = ("gx_0", "gx_1", "gy_0", "gy_1", "gz")
+    split = Mesh(mesh.devices.reshape(4, 2, 2, 4, mesh.shape["gz"]), axes)
     return jax.shard_map(
         local,
         mesh=split,

time: 108 us -> 98.5 us (0.912); the launches traced: 106 us -> 99 us
  blocking collectives: 63.9 us -> 75.1 us
  Pallas kernels: 21.7 us -> 13.9 us
  waiting for transfers between devices: 8.13 us -> 2.76 us
  starting transfers between devices: 6.15 us -> 4.25 us
  other arithmetic: 3.08 us -> 1.2 us
  local copies, waits for them, and re-layouts: 2.79 us -> 1.68 us
    all_to_all x2 -> x3, blocking collectives: 35.7 us -> 50.4 us  [the longest x1 18.8 us: local(): pieces = lax.all_to_all(plane, ('gy_0', 'gy_1'), 0, 0, tiled=True)]
    pallas_call x1, Pallas kernels: 21.7 us -> 13.6 us  [local_products(): pl.pallas_call(local_kernel, grid_spec=pltpu.PrefetchScalarGridSpec(num_s...]
    all_to_all x1 -> x0, starting transfers between devices: 6.15 us -> none  [local(): gathered = lax.all_to_all(copies, ('gx_0', 'gx_1'), 0, 0, tiled=True)]
    all_to_all x1 -> x0, waiting for transfers between devices: 4.8 us -> none  [local(): gathered = lax.all_to_all(copies, ('gx_0', 'gx_1'), 0, 0, tiled=True)]
    ppermute x1, starting transfers between devices: 0.01 us -> 4.25 us  [local(): arrived = lax.ppermute(sent, 'gx_1', [(0, 1), (1, 0)])]
    all_to_all x1, blocking collectives: 28.3 us -> 24.7 us  [local(): lax.all_to_all(pair.reshape(16, 2 * ROWS, LANES), ('gx_0', 'gz'), 0, 0, t...]
    convert_element_type x1, other arithmetic: 2.09 us -> 0.32 us  [local(): pair = (kept + arrived.astype(F32)).astype(BF16)]
  transfers between devices with their start and end apart: 2 -> 1, of which waited for: 2 -> 1; matrix products, arithmetic and copies ran while one was open for 0% -> 0% of each run, Pallas kernels for 0% -> 0%
where the time goes in v2:
time: 98.5 us; the launch traced here: 99 us
  blocking collectives  75.1 us (76%)
  Pallas kernels  13.9 us (14%)
  starting transfers between devices  4.25 us (4%)
  waiting for transfers between devices  2.76 us (3%)
  local copies, waits for them, and re-layouts  1.68 us (2%)
  other arithmetic  1.2 us (1%)
    all_to_all x1, blocking collectives, local(): lax.all_to_all(pair.reshape(16, 2 * ROWS, LANES), ('gx_0', 'gz'), 0, 0, t...  24.7 us
    all_to_all x1, blocking collectives, local(): pieces = lax.all_to_all(plane, ('gy_0', 'gy_1'), 0, 0, tiled=True)  18.8 us
    all_to_all x1, blocking collectives, local(): lax.all_to_all(copies, ('gx_0', 'gx_1', 'gy_0'), 0, 0, tiled=True)  16.1 us
    all_to_all x1, blocking collectives, local(): lax.all_to_all(gram_part(rounded, gathered), ('gy_1', 'gz'), 0, 0, tiled=...  15.5 us
    pallas_call x1, Pallas kernels, local_products(): pl.pallas_call(local_kernel, grid_spec=pltpu.PrefetchScalarGridSpec(num_s...  13.6 us
    ppermute x1, starting transfers between devices, local(): arrived = lax.ppermute(sent, 'gx_1', [(0, 1), (1, 0)])  4.25 us
    ppermute x1, waiting for transfers between devices, local(): arrived = lax.ppermute(sent, 'gx_1', [(0, 1), (1, 0)])  2.76 us
  transfers between devices with their start and end apart: 1, of which 1 were waited for; matrix products, arithmetic and copies ran while one was open for 0% of the time, Pallas kernels for 0%

profile of v2, /device:TPU:1, one launch (start us, length us, event | category | flops | bytes accessed | tf_op | source)
XLA Modules:
  0.0 99.0 jit_solution(12239062985118145815)
XLA Ops:
  0.0 0.0 copy-start
  0.0 0.9 copy-done
  0.9 0.0 copy-start.1
  0.9 0.7 copy-done.1
  1.6 13.6 %local_products.1 = (f32[4,4,2,168,128]{4,3,2,1,0:T(8,128)S(1)}, bf16[4,4,2,168,128]{4,3,2,1,0:T(8,128)(2,1)S(1)}) custom-call(s32[3,6]{1,0:T(4,128)S(1)} %bitcast.9, s32[1]{0:T(128)} %bitcast.1.core, bf16[6,64,4096]{2,1,0:T(8,128)(2,1)} %stored.1, bf16[48,1024]{1,0:T(8,128)(2,1)S(1)} %bitcast.8), custom_call_target="tpu_custom_call" | custom-call | tf_op jit(solution)/shard_map/local_products/pallas_call | solution.py:195
  15.2 4.3 %collective-permute-start = (bf16[4,4,2,168,128]{4,3,2,1,0:T(8,128)(2,1)S(1)}, bf16[4,4,2,168,128]{4,3,2,1,0:T(8,128)(2,1)S(1)}, u32[]{:S(2)}, u32[]{:S(2)}) collective-permute-start(bf16[4,4,2,168,128]{4,3,2,1,0:T(8,128)(2,1)S(1)} %get-tuple-element.8), channel_id=1, source_target_pairs={{0,32},{32,0},{1,33},{33,1},{2,34},{34,2},{3,35},{35,3},{4,36},{36... | collective-permute-start | bytes 4128776 | tf_op jit(solution)/shard_map/ppermute | solution.py:256
  19.4 2.8 %collective-permute-done = bf16[4,4,2,168,128]{4,3,2,1,0:T(8,128)(2,1)S(1)} collective-permute-done((bf16[4,4,2,168,128]{4,3,2,1,0:T(8,128)(2,1)S(1)}, bf16[4,4,2,168,128]{4,3,2,1,0:T(8,128)(2,1)S(1)}, u32[]{:S(2)}, u32[]{:S(2)}) %collective-permute-start) | collective-permute-done | bytes 1376288 | tf_op jit(solution)/shard_map/ppermute | solution.py:256
  22.2 0.3 add_convert_fusion
  22.5 24.7 %all_to_all.20 = bf16[16,336,128]{2,1,0:T(8,128)(2,1)S(1)} all-to-all(bf16[16,336,128]{2,1,0:T(8,128)(2,1)S(1)} %bitcast.10), channel_id=1, replica_groups=mesh['gx_0'=4,'gx_1'=2,'gy_0'=2,'gy_1'=4,'gz'=4] {'gx_0','gz'}, dimensions={0} | all-to-all | bytes 2752512 | tf_op jit(solution)/shard_map/all_to_all | solution.py:258
  47.2 0.2 convert_reduce_fusion
  47.5 18.8 %all_to_all.21 = f32[8,42,128]{2,1,0:T(8,128)S(1)} all-to-all(f32[8,42,128]{2,1,0:T(8,128)S(1)} %copy.6), channel_id=1, replica_groups=mesh['gx_0'=4,'gx_1'=2,'gy_0'=2,'gy_1'=4,'gz'=4] {'gy_0','gy_1'}, dimensions={0} | all-to-all | bytes 344064 | tf_op jit(solution)/shard_map/all_to_all | solution.py:264
  66.4 16.1 %all_to_all.22.gathered = bf16[16,42,128]{2,1,0:T(8,128)(2,1)S(1)} all-to-all(bf16[16,42,128]{2,1,0:T(8,128)(2,1)S(1)} %broadcast_in_dim.3), channel_id=1, replica_groups=mesh['gx_0'=4,'gx_1'=2,'gy_0'=2,'gy_1'=4,'gz'=4] {'gx_0','gx_1','gy_0'}, dimensions={0} | all-to-all | bytes 344064 | tf_op jit(solution)/shard_map/all_to_all | solution.py:267
  82.5 0.3 gram_part.1
  82.8 15.5 %all_to_all.23 = f32[16,4,1024]{2,1,0:T(4,128)S(1)} all-to-all(f32[16,4,1024]{2,1,0:T(4,128)S(1)} %gram_part.1), channel_id=1, replica_groups=mesh['gx_0'=4,'gx_1'=2,'gy_0'=2,'gy_1'=4,'gz'=4] {'gy_1','gz'}, dimensions={0} | all-to-all | bytes 524288 | tf_op jit(solution)/shard_map/all_to_all | solution.py:268
  98.3 0.1 reduce_sum.29
  98.4 0.6 broadcast_multiply_fusion
  (4 shorter events, 0.1 us)
Async XLA Ops:
  0.0 0.9 copy-start
  0.9 0.7 copy-start.1
  15.2 7.0 %collective-permute-start = (bf16[4,4,2,168,128]{4,3,2,1,0:T(8,128)(2,1)S(1)}, bf16[4,4,2,168,128]{4,3,2,1,0:T(8,128)(2,1)S(1)}, u32[]{:S(2)}, u32[]{:S(2)}) collective-permute-start(bf16[4,4,2,168,128]{4,3,2,1,0:T(8,128)(2,1)S(1)} %get-tuple-element.8), channel_id=1, source_target_pairs={{0,32},{32,0},{1,33},{33,1},{2,34},{34,2},{3,35},{35,3},{4,36},{36... | collective-permute-start | bytes 4128776 | tf_op jit(solution)/shard_map/ppermute | solution.py:256

commit v3 on v2

--- a/solution.py
+++ b/solution.py
@@ -187,6 +187,10 @@
             return carry
 
         lax.fori_loop(0, NB // 2, write, 0)
+
+
+def in_hbm(array):
+    return pltpu.with_memory_space_constraint(array, pltpu.HBM)
 
 
 def local_products(blocks, ownership, basis, core):
@@ -215,27 +219,19 @@
         out_shape=[jax.ShapeDtypeStruct(half, F32), jax.ShapeDtypeStruct(half, BF16)],
         compiler_params=pltpu.CompilerParams(vmem_limit_bytes=48 << 20),
         name="local_products",
-    )(ownership.T, core, blocks, basis)
+    )(in_hbm(ownership.T), core, blocks, in_hbm(basis))
 
 
 def gram_kernel(mine, gathered, out):
-    depth = mine.shape[0]
-    low = lax.broadcasted_iota(jnp.int32, (depth, LANES), 1) < BS
-    pair = lax.broadcasted_iota(jnp.int32, (depth, LANES), 0) // 2
+    pair = lax.broadcasted_iota(jnp.int32, mine.shape, 0)
+    pair = jnp.where(pair < TRI, pair, pair - TRI)
     on_diagonal = pair < 0
     for q in range(QB):
         on_diagonal = on_diagonal | (pair == q * (q + 3) // 2)
     weighted = (mine[...].astype(F32) * jnp.where(on_diagonal, 1.0, 2.0)).astype(BF16)
-    lows = []
-    highs = []
-    for g in range(0, NB, 2):
-        first = gathered[g].astype(F32)
-        second = gathered[g + 1].astype(F32)
-        lows.append(jnp.where(low, first, pltpu.roll(second, BS, 1)).astype(BF16))
-        highs.append(jnp.where(low, pltpu.roll(first, BS, 1), second).astype(BF16))
-    gram = dot(weighted[:, :BS], jnp.concatenate(lows, 1), TN)
-    gram = gram + dot(weighted[:, BS:], jnp.concatenate(highs, 1), TN)
-    for i in range(16):
+    everyone = jnp.concatenate([gathered[g] for g in range(gathered.shape[0])], 1)
+    gram = dot(weighted, everyone, TN)
+    for i in range(out.shape[0]):
         out[i] = gram[4 * i : 4 * i + 4].astype(out.dtype)
 
 
@@ -244,10 +240,32 @@
         gram_kernel,
         in_specs=[pl.BlockSpec(memory_space=pltpu.VMEM)] * 2,
         out_specs=pl.BlockSpec(memory_space=pltpu.VMEM),
-        out_shape=jax.ShapeDtypeStruct((16, 4, NB * BS), F32),
+        out_shape=jax.ShapeDtypeStruct((32, 4, NB * BS), BF16),
         compiler_params=pltpu.CompilerParams(vmem_limit_bytes=16 << 20),
         name="gram_part",
     )(mine, gathered)
+
+
+def merge_kernel(pieces, out):
+    total = pieces[0]
+    for i in range(1, pieces.shape[0]):
+        total = total + pieces[i]
+    low = lax.broadcasted_iota(jnp.int32, (TRI, LANES), 1) < BS
+    first = total[:TRI]
+    second = total[TRI:]
+    out[:TRI] = jnp.where(low, first, pltpu.roll(second, BS, 1)).astype(BF16)
+    out[TRI:] = jnp.where(low, pltpu.roll(first, BS, 1), second).astype(BF16)
+
+
+def merged(pieces):
+    return pl.pallas_call(
+        merge_kernel,
+        in_specs=[pl.BlockSpec(memory_space=pltpu.VMEM)],
+        out_specs=pl.BlockSpec(memory_space=pltpu.VMEM),
+        out_shape=jax.ShapeDtypeStruct((2 * TRI, LANES), BF16),
+        compiler_params=pltpu.CompilerParams(vmem_limit_bytes=16 << 20),
+        name="merged",
+    )(pieces)
 
 
 def local(blocks, ownership, basis_rows):
@@ -259,19 +277,18 @@
         pair.reshape(16, 2 * ROWS, LANES), ("gx_0", "gz"), 0, 0, tiled=True
     )
     plane = pieces.astype(F32).sum(axis=0)
-    plane = plane.reshape(2, TRI, 4, 2, LANES).transpose(0, 2, 1, 3, 4)
-    plane = plane.reshape(8, 2 * TRI, LANES)
-    pieces = lax.all_to_all(plane, ("gy_0", "gy_1"), 0, 0, tiled=True)
-    rounded = pieces.sum(axis=0).astype(BF16)
-    copies = jnp.broadcast_to(rounded, (16, 2 * TRI, LANES))
-    gathered = lax.all_to_all(copies, ("gx_0", "gx_1", "gy_0"), 0, 0, tiled=True)
-    pieces = lax.all_to_all(gram_part(rounded, gathered), ("gy_1", "gz"), 0, 0, tiled=True)
-    return pieces.sum(axis=0) / R
+    plane = plane.reshape(2 * TRI, BLK, LANES).swapaxes(0, 1)
+    pieces = lax.all_to_all(plane, "gy", 0, 0, tiled=True)
+    rounded = merged(pieces)
+    copies = jnp.broadcast_to(rounded, (8, 2 * TRI, LANES))
+    gathered = lax.all_to_all(copies, ("gx_0", "gx_1"), 0, 0, tiled=True)
+    pieces = lax.all_to_all(gram_part(rounded, gathered), ("gy", "gz"), 0, 0, tiled=True)
+    return pieces.astype(F32).sum(axis=0) / R
 
 
 def solution(mesh):
-    axes = ("gx_0", "gx_1", "gy_0", "gy_1", "gz")
-    split = Mesh(mesh.devices.reshape(4, 2, 2, 4, mesh.shape["gz"]), axes)
+    axes = ("gx_0", "gx_1", "gy", "gz")
+    split = Mesh(mesh.devices.reshape(4, 2, mesh.shape["gy"], mesh.shape["gz"]), axes)
     return jax.shard_map(
         local,
         mesh=split,

time: 98.5 us -> 90.2 us (0.916)
  starting transfers between devices: 4.25 us -> 0.09 us
  blocking collectives: 75.1 us -> 71.2 us
  local copies, waits for them, and re-layouts: 1.68 us -> 0.05 us
    all_to_all x3, blocking collectives: 50.4 us -> 40.4 us  [the longest x1 15.7 us: local(): pieces = lax.all_to_all(plane, 'gy', 0, 0, tiled=True)]
    all_to_all x1, blocking collectives: 24.7 us -> 30.8 us  [local(): lax.all_to_all(pair.reshape(16, 2 * ROWS, LANES), ('gx_0', 'gz'), 0, 0, t...]
    ppermute x1, starting transfers between devices: 4.25 us -> 0.09 us  [local(): arrived = lax.ppermute(sent, 'gx_1', [(0, 1), (1, 0)])]
    unnamed x4 -> x0, local copies, waits for them, and re-layouts: 1.57 us -> none
where the time goes in v3:
time: 90.2 us; the launch traced here: 89.8 us
  blocking collectives  71.2 us (79%)
  Pallas kernels  14.1 us (16%)
  waiting for transfers between devices  3.12 us (3%)
  other arithmetic  1.2 us (1%)
    all_to_all x1, blocking collectives, local(): lax.all_to_all(pair.reshape(16, 2 * ROWS, LANES), ('gx_0', 'gz'), 0, 0, t...  30.8 us
    all_to_all x1, blocking collectives, local(): pieces = lax.all_to_all(plane, 'gy', 0, 0, tiled=True)  15.7 us
    all_to_all x1, blocking collectives, local(): lax.all_to_all(gram_part(rounded, gathered), ('gy', 'gz'), 0, 0, tiled=True)  14.4 us
    pallas_call x1, Pallas kernels, local_products(): pl.pallas_call(local_kernel, grid_spec=pltpu.PrefetchScalarGridSpec(num_s...  13.7 us
    all_to_all x1, blocking collectives, local(): gathered = lax.all_to_all(copies, ('gx_0', 'gx_1'), 0, 0, tiled=True)  10.2 us
    ppermute x1, waiting for transfers between devices, local(): arrived = lax.ppermute(sent, 'gx_1', [(0, 1), (1, 0)])  3.12 us
  transfers between devices with their start and end apart: 1, of which 1 were waited for; matrix products, arithmetic and copies ran while one was open for 0% of the time, Pallas kernels for 0%

profile of v3, /device:TPU:1, one launch (start us, length us, event | category | flops | bytes accessed | tf_op | source)
XLA Modules:
  0.0 89.8 jit_solution(5690958097555047042)
XLA Ops:
  0.0 13.7 %local_products.1 = (f32[4,4,2,168,128]{4,3,2,1,0:T(8,128)S(1)}, bf16[4,4,2,168,128]{4,3,2,1,0:T(8,128)(2,1)S(1)}) custom-call(s32[3,6]{1,0:T(4,128)} %bitcast.12, s32[1]{0:T(128)} %bitcast.1.core, bf16[6,64,4096]{2,1,0:T(8,128)(2,1)} %stored.1, bf16[48,1024]{1,0:T(8,128)(2,1)} %bitcast.11), custom_call_target="tpu_custom_call" | custom-call | tf_op jit(solution)/shard_map/local_products/pallas_call | solution.py:199
  13.7 0.1 collective-permute-start
  13.8 3.1 %collective-permute-done = bf16[4,4,2,168,128]{4,3,2,1,0:T(8,128)(2,1)S(1)} collective-permute-done((bf16[4,4,2,168,128]{4,3,2,1,0:T(8,128)(2,1)S(1)}, bf16[4,4,2,168,128]{4,3,2,1,0:T(8,128)(2,1)S(1)}, u32[]{:S(2)}, u32[]{:S(2)}) %collective-permute-start) | collective-permute-done | bytes 1376288 | tf_op jit(solution)/shard_map/ppermute | solution.py:274
  17.0 0.3 add_convert_fusion
  17.2 30.8 %all_to_all.20 = bf16[16,336,128]{2,1,0:T(8,128)(2,1)S(1)} all-to-all(bf16[16,336,128]{2,1,0:T(8,128)(2,1)S(1)} %bitcast.8), channel_id=1, replica_groups=mesh['gx_0'=4,'gx_1'=2,'gy'=8,'gz'=4] {'gx_0','gz'}, dimensions={0} | all-to-all | bytes 2752512 | tf_op jit(solution)/shard_map/all_to_all | solution.py:276
  48.0 0.2 convert_reduce_fusion
  48.3 15.7 %all_to_all.21.pieces = f32[8,42,128]{2,1,0:T(8,128)S(1)} all-to-all(f32[8,42,128]{2,1,0:T(8,128)S(1)} %bitcast.9), channel_id=1, replica_groups=mesh['gx_0'=4,'gx_1'=2,'gy'=8,'gz'=4] {'gy'}, dimensions={0} | all-to-all | bytes 344064 | tf_op jit(solution)/shard_map/all_to_all | solution.py:281
  64.0 0.1 merged.1.mine
  64.1 10.2 %all_to_all.22.gathered = bf16[8,42,128]{2,1,0:T(8,128)(2,1)S(1)} all-to-all(bf16[8,42,128]{2,1,0:T(8,128)(2,1)S(1)} %broadcast_in_dim.3), channel_id=1, replica_groups=mesh['gx_0'=4,'gx_1'=2,'gy'=8,'gz'=4] {'gx_0','gx_1'}, dimensions={0} | all-to-all | bytes 172032 | tf_op jit(solution)/shard_map/all_to_all | solution.py:284
  74.4 0.3 gram_part.1
  74.6 14.4 %all_to_all.23 = bf16[32,4,1024]{2,1,0:T(4,128)(2,1)S(1)} all-to-all(bf16[32,4,1024]{2,1,0:T(4,128)(2,1)S(1)} %gram_part.1), channel_id=1, replica_groups=mesh['gx_0'=4,'gx_1'=2,'gy'=8,'gz'=4] {'gy','gz'}, dimensions={0} | all-to-all | bytes 524288 | tf_op jit(solution)/shard_map/all_to_all | solution.py:285
  89.1 0.1 convert_reduce_fusion.1
  89.2 0.6 broadcast_multiply_fusion
  (2 shorter events, 0.1 us)
Async XLA Ops:
  13.7 3.2 %collective-permute-start = (bf16[4,4,2,168,128]{4,3,2,1,0:T(8,128)(2,1)S(1)}, bf16[4,4,2,168,128]{4,3,2,1,0:T(8,128)(2,1)S(1)}, u32[]{:S(2)}, u32[]{:S(2)}) collective-permute-start(bf16[4,4,2,168,128]{4,3,2,1,0:T(8,128)(2,1)S(1)} %get-tuple-element.8), channel_id=1, source_target_pairs={{0,32},{32,0},{1,33},{33,1},{2,34},{34,2},{3,35},{35,3},{4,36},{36... | collective-permute-start | bytes 4128776 | tf_op jit(solution)/shard_map/ppermute | solution.py:274

commit v4 on v3

--- a/solution.py
+++ b/solution.py
@@ -21,6 +21,12 @@
 F32 = jnp.float32
 BF16 = jnp.bfloat16
 
+ORDER_Y = (2, 3, 0, 1)
+ORDER_X = (2, 0, 3, 1)
+ORDER_Z = (4, 5, 6, 7, 0, 1, 2, 3)
+ORDER_YC = (4, 5, 6, 7, 0, 1, 2, 3)
+ORDER_ZX = tuple(4 * z + x for z in ORDER_Z for x in ORDER_X)
+
 NN = (((1,), (0,)), ((), ()))
 NT = (((1,), (1,)), ((), ()))
 TN = (((0,), (0,)), ((), ()))
@@ -31,7 +37,7 @@
 
 
 def local_kernel(
-    own, core, stored, basis, keep, send, acc, bases, masked, swapped, wide, with_y, with_x
+    own, core, stored, basis, acc, send, bases, masked, swapped, wide, wide1, wide0, wide2, with_y, with_x
 ):
     slot = pl.program_id(0)
 
@@ -48,8 +54,8 @@
             jnp.where(mask, pltpu.roll(first, BS, 1), second),
         )
 
-    def row_of_each(row, count=HALF):
-        return wide[pl.ds(row, count, stride=STRIDE), :]
+    def row_of_each(ref, row, count=HALF):
+        return ref[pl.ds(row, count, stride=STRIDE), :]
 
     @pl.when(slot == 0)
     def _():
@@ -96,14 +102,13 @@
             lane = lax.broadcasted_iota(jnp.int32, (BS, LANES), 1)
             z = lane & (BS - 1)
             y_high = jnp.where(lane < BS, 0, HALF)
+            order_xy = jnp.where(front, (y_high - x).astype(F32) * 0.5 + 0.5, 2.0 * BS)
+            order_yz = jnp.where(back, (z - y_high).astype(F32) * 0.5 + 0.5, 2.0 * BS)
 
             def scale(i, carry):
-                y = y_high + i
-                dxy = jnp.where(front, x - y, -1)
-                dyz = jnp.where(back, y - z, -1)
-                w = jnp.where(dxy == 0, 0.5, 1.0) * jnp.where(dyz == 0, 0.5, 1.0)
-                w = jnp.where((dxy == 0) & (dyz == 0), 1.0 / 6.0, w)
-                w = jnp.where((dxy > 0) | (dyz > 0), 0.0, w)
+                step = i.astype(F32) * 0.5
+                w = jnp.clip(order_xy + step, 0.0, 1.0) * jnp.clip(order_yz - step, 0.0, 1.0)
+                w = jnp.where(w == 0.25, 1.0 / 6.0, w)
                 rows = pl.ds(i * STRIDE, BS)
                 scaled = wide[rows, :] * w
                 wide[rows, :] = scaled
@@ -113,39 +118,48 @@
             lax.fori_loop(0, HALF, scale, 0, unroll=4)
 
         for i in range(HALF):
-            upper, lower = paired(row_of_each(i), row_of_each(i + HALF))
+            upper, lower = paired(row_of_each(wide, i), row_of_each(wide, i + HALF))
             swapped[:HALF, tile(i)] = upper.astype(BF16)
             swapped[HALF:, tile(i)] = lower.astype(BF16)
 
-        def spread(values, target, place):
+        def spread(values, ref, target, place):
             for i in range(HALF):
-                wide[i * STRIDE : i * STRIDE + R, :] = values[:, tile(i)]
+                ref[i * STRIDE : i * STRIDE + R, :] = values[:, tile(i)]
             for j in range(PAIRS):
-                upper, lower = paired(row_of_each(2 * j), row_of_each(2 * j + 1))
+                upper, lower = paired(row_of_each(ref, 2 * j), row_of_each(ref, 2 * j + 1))
                 target[:HALF, tile(place(j))] = upper.astype(BF16)
                 target[HALF:, tile(place(j))] = lower.astype(BF16)
 
-        spread(dot(u1, swapped[...]), with_x, lambda j: j)
-        spread(dot(u0, masked[...]), with_y, lambda j: 2 * j + 1)
+        spread(dot(u1, swapped[...]), wide1, with_x, lambda j: j)
+        spread(dot(u0, masked[...]), wide0, with_y, lambda j: 2 * j + 1)
         for i in range(QUARTER):
             both_tiles = [masked[:, tile(i)], masked[:, tile(i + QUARTER)]]
-            wide[i * STRIDE : i * STRIDE + 2 * R, :] = dot(
+            wide2[i * STRIDE : i * STRIDE + 2 * R, :] = dot(
                 both2, jnp.concatenate(both_tiles, 0), NT
             )
         for j in range(PAIRS):
             for k in range(2):
                 parts = paired(
-                    row_of_each(k * R + 2 * j, QUARTER), row_of_each(k * R + 2 * j + 1, QUARTER)
+                    row_of_each(wide2, k * R + 2 * j, QUARTER),
+                    row_of_each(wide2, k * R + 2 * j + 1, QUARTER),
                 )
                 for h in range(2):
                     top = (2 * k + h) * QUARTER
                     with_y[top : top + QUARTER, tile(2 * j)] = parts[h].astype(BF16)
 
-        def add(block, j, value):
+        def place(v):
+            group = sum(jnp.where(v // 4 == y, i, 0) for i, y in enumerate(ORDER_Y))
+            return ((v // 2) % 2) ^ core[0], group, v % 2
+
+        places = [place(v) for v in (v0, v1, v2)]
+
+        def add(f, j, value):
+            side, group, half = places[f]
+            block = (side, group, j % 4, half)
             q = j // 4
             start = BLK * (q * (q + 1) // 2)
             rows = BLK * (q + 1)
-            at = (block, j % 4, slice(start, start + rows), slice(None))
+            at = (*block, slice(start, start + rows), slice(None))
             acc[at] = acc[at] + value[:rows]
 
         def stacked(ref, tiles):
@@ -172,21 +186,17 @@
                 for h in range(2):
                     i = 2 * k + h
                     j = 8 * g + i
-                    add(v0, j, over_y[:, tile(2 * i)] + from_x[h])
-                    add(v1, j, from_y[h])
-                    add(v2, j, over_y[:, tile(2 * i + 1)] + over_x[:, tile(i)])
+                    add(0, j, over_y[:, tile(2 * i)] + from_x[h])
+                    add(1, j, from_y[h])
+                    add(2, j, over_y[:, tile(2 * i + 1)] + over_x[:, tile(i)])
 
     @pl.when(slot == pl.num_programs(0) - 1)
     def _():
-        mine = core[0]
-
         def write(m, carry):
-            block = 4 * (m // 2) + m % 2
-            keep[m // 2, :, m % 2] = acc[block + 2 * mine]
-            send[m // 2, :, m % 2] = acc[block + 2 * (1 - mine)].astype(BF16)
+            send[m] = acc[1, m].astype(BF16)
             return carry
 
-        lax.fori_loop(0, NB // 2, write, 0)
+        lax.fori_loop(0, 4, write, 0)
 
 
 def in_hbm(array):
@@ -207,19 +217,24 @@
             ],
             out_specs=[pl.BlockSpec(memory_space=pltpu.VMEM)] * 2,
             scratch_shapes=[
-                pltpu.VMEM((NB, 4, ROWS, LANES), F32),
                 pltpu.VMEM((NB, R, BS), BF16),
                 pltpu.VMEM((BS, BS * BS), BF16),
                 pltpu.VMEM((BS, BS * BS), BF16),
                 pltpu.VMEM((HALF * STRIDE, LANES), F32),
+                pltpu.VMEM((HALF * STRIDE, LANES), F32),
+                pltpu.VMEM((HALF * STRIDE, LANES), F32),
+                pltpu.VMEM((QUARTER * STRIDE, LANES), F32),
                 pltpu.VMEM((BS, 2 * PAIRS * LANES), BF16),
                 pltpu.VMEM((BS, PAIRS * LANES), BF16),
             ],
         ),
-        out_shape=[jax.ShapeDtypeStruct(half, F32), jax.ShapeDtypeStruct(half, BF16)],
-        compiler_params=pltpu.CompilerParams(vmem_limit_bytes=48 << 20),
+        out_shape=[
+            jax.ShapeDtypeStruct((2, *half), F32),
+            jax.ShapeDtypeStruct(half, BF16),
+        ],
+        compiler_params=pltpu.CompilerParams(vmem_limit_bytes=36 << 20),
         name="local_products",
-    )(in_hbm(ownership.T), core, blocks, in_hbm(basis))
+    )(in_hbm(ownership.T), core, in_hbm(blocks), in_hbm(basis))
 
 
 def gram_kernel(mine, gathered, out):
@@ -229,10 +244,10 @@
     for q in range(QB):
         on_diagonal = on_diagonal | (pair == q * (q + 3) // 2)
     weighted = (mine[...].astype(F32) * jnp.where(on_diagonal, 1.0, 2.0)).astype(BF16)
-    everyone = jnp.concatenate([gathered[g] for g in range(gathered.shape[0])], 1)
-    gram = dot(weighted, everyone, TN)
-    for i in range(out.shape[0]):
-        out[i] = gram[4 * i : 4 * i + 4].astype(out.dtype)
+    everyone = jnp.concatenate([gathered[ORDER_YC.index(g)] for g in range(len(ORDER_YC))], 1)
+    gram = dot(weighted, everyone, TN) / R
+    for i, place in enumerate(ORDER_ZX):
+        out[i] = gram[4 * place : 4 * place + 4].astype(out.dtype)
 
 
 def gram_part(mine, gathered):
@@ -246,44 +261,53 @@
     )(mine, gathered)
 
 
-def merge_kernel(pieces, out):
+def merge_kernel(pieces, out, copies):
     total = pieces[0]
     for i in range(1, pieces.shape[0]):
         total = total + pieces[i]
     low = lax.broadcasted_iota(jnp.int32, (TRI, LANES), 1) < BS
     first = total[:TRI]
     second = total[TRI:]
-    out[:TRI] = jnp.where(low, first, pltpu.roll(second, BS, 1)).astype(BF16)
-    out[TRI:] = jnp.where(low, pltpu.roll(first, BS, 1), second).astype(BF16)
+    upper = jnp.where(low, first, pltpu.roll(second, BS, 1)).astype(BF16)
+    lower = jnp.where(low, pltpu.roll(first, BS, 1), second).astype(BF16)
+    for ref in (out, *(copies.at[g] for g in range(copies.shape[0]))):
+        ref[:TRI] = upper
+        ref[TRI:] = lower
 
 
 def merged(pieces):
     return pl.pallas_call(
         merge_kernel,
         in_specs=[pl.BlockSpec(memory_space=pltpu.VMEM)],
-        out_specs=pl.BlockSpec(memory_space=pltpu.VMEM),
-        out_shape=jax.ShapeDtypeStruct((2 * TRI, LANES), BF16),
+        out_specs=[pl.BlockSpec(memory_space=pltpu.VMEM)] * 2,
+        out_shape=[
+            jax.ShapeDtypeStruct((2 * TRI, LANES), BF16),
+            jax.ShapeDtypeStruct((8, 2 * TRI, LANES), BF16),
+        ],
         compiler_params=pltpu.CompilerParams(vmem_limit_bytes=16 << 20),
         name="merged",
     )(pieces)
+
+
+def exchange(pieces, axes, order):
+    return lax.all_to_all(
+        pieces, axes, 0, 0, axis_index_groups=[list(order)], tiled=True
+    )
 
 
 def local(blocks, ownership, basis_rows):
     core = lax.axis_index("gx_1").astype(jnp.int32).reshape(1)
     kept, sent = local_products(blocks, ownership, basis_rows.T, core)
     arrived = lax.ppermute(sent, "gx_1", [(0, 1), (1, 0)])
-    pair = (kept + arrived.astype(F32)).astype(BF16)
-    pieces = lax.all_to_all(
-        pair.reshape(16, 2 * ROWS, LANES), ("gx_0", "gz"), 0, 0, tiled=True
-    )
+    pair = (kept[0] + arrived.astype(F32)).astype(BF16)
+    ranks = [4 * y + x for y in ORDER_Y for x in ORDER_X]
+    pieces = exchange(pair.reshape(16, 2 * ROWS, LANES), ("gx_0", "gz"), ranks)
     plane = pieces.astype(F32).sum(axis=0)
     plane = plane.reshape(2 * TRI, BLK, LANES).swapaxes(0, 1)
-    pieces = lax.all_to_all(plane, "gy", 0, 0, tiled=True)
-    rounded = merged(pieces)
-    copies = jnp.broadcast_to(rounded, (8, 2 * TRI, LANES))
-    gathered = lax.all_to_all(copies, ("gx_0", "gx_1"), 0, 0, tiled=True)
-    pieces = lax.all_to_all(gram_part(rounded, gathered), ("gy", "gz"), 0, 0, tiled=True)
-    return pieces.astype(F32).sum(axis=0) / R
+    rounded, copies = merged(exchange(plane, "gy", ORDER_Z))
+    gathered = exchange(copies, ("gx_0", "gx_1"), ORDER_YC)
+    pieces = exchange(gram_part(rounded, gathered), ("gy", "gz"), ORDER_ZX)
+    return pieces.astype(F32).sum(axis=0)
 
 
 def solution(mesh):

time: 90.2 us -> 85.2 us (0.945)
  blocking collectives: 71.2 us -> 63.5 us
  starting transfers between devices: 0.09 us -> 3.3 us
    all_to_all x4, blocking collectives: 71.2 us -> 63.5 us  [exchange(): lax.all_to_all(pieces, axes, 0, 0, axis_index_groups=[list(order)], tiled...]
    ppermute x1, starting transfers between devices: 0.09 us -> 3.3 us  [local(): arrived = lax.ppermute(sent, 'gx_1', [(0, 1), (1, 0)])]
where the time goes in v4:
time: 85.2 us; the launch traced here: 85.1 us
  blocking collectives  63.5 us (75%)
  Pallas kernels  14.3 us (17%)
  starting transfers between devices  3.3 us (4%)
  waiting for transfers between devices  2.76 us (3%)
  other arithmetic  1.19 us (1%)
    all_to_all x4, blocking collectives, exchange(): lax.all_to_all(pieces, axes, 0, 0, axis_index_groups=[list(order)], tiled...  63.5 us
    pallas_call x1, Pallas kernels, local_products(): pl.pallas_call(local_kernel, grid_spec=pltpu.PrefetchScalarGridSpec(num_s...  13.9 us
    ppermute x1, starting transfers between devices, local(): arrived = lax.ppermute(sent, 'gx_1', [(0, 1), (1, 0)])  3.3 us
    ppermute x1, waiting for transfers between devices, local(): arrived = lax.ppermute(sent, 'gx_1', [(0, 1), (1, 0)])  2.76 us
  transfers between devices with their start and end apart: 1, of which 1 were waited for; matrix products, arithmetic and copies ran while one was open for 0% of the time, Pallas kernels for 0%

profile of v4, /device:TPU:1, one launch (start us, length us, event | category | flops | bytes accessed | tf_op | source)
XLA Modules:
  0.0 85.1 jit_solution(4611501931086376846)
XLA Ops:
  0.0 13.9 %local_products.1 = (f32[2,4,4,2,168,128]{5,4,3,2,1,0:T(8,128)S(1)}, bf16[4,4,2,168,128]{4,3,2,1,0:T(8,128)(2,1)S(1)}) custom-call(s32[3,6]{1,0:T(4,128)} %bitcast.16, s32[1]{0:T(128)} %bitcast.1.core, bf16[6,64,4096]{2,1,0:T(8,128)(2,1)} %stored.1, bf16[48,1024]{1,0:T(8,128)(2,1)} %bitcast.15), custom_call_target="tpu_custom_call" | custom-call | tf_op jit(solution)/shard_map/local_products/pallas_call | solution.py:209
  13.9 3.3 %collective-permute-start = (bf16[4,4,2,168,128]{4,3,2,1,0:T(8,128)(2,1)S(1)}, bf16[4,4,2,168,128]{4,3,2,1,0:T(8,128)(2,1)S(1)}, u32[]{:S(2)}, u32[]{:S(2)}) collective-permute-start(bf16[4,4,2,168,128]{4,3,2,1,0:T(8,128)(2,1)S(1)} %get-tuple-element.10), channel_id=1, source_target_pairs={{0,32},{32,0},{1,33},{33,1},{2,34},{34,2},{3,35},{35,3},{4,36},{36... | collective-permute-start | bytes 4128776 | tf_op jit(solution)/shard_map/ppermute | solution.py:301
  17.2 2.8 %collective-permute-done = bf16[4,4,2,168,128]{4,3,2,1,0:T(8,128)(2,1)S(1)} collective-permute-done((bf16[4,4,2,168,128]{4,3,2,1,0:T(8,128)(2,1)S(1)}, bf16[4,4,2,168,128]{4,3,2,1,0:T(8,128)(2,1)S(1)}, u32[]{:S(2)}, u32[]{:S(2)}) %collective-permute-start) | collective-permute-done | bytes 1376288 | tf_op jit(solution)/shard_map/ppermute | solution.py:301
  20.0 0.3 fusion
  20.2 23.3 %all_to_all.20 = bf16[16,336,128]{2,1,0:T(8,128)(2,1)S(1)} all-to-all(bf16[16,336,128]{2,1,0:T(8,128)(2,1)S(1)} %bitcast.12), channel_id=1, replica_groups={{130,128,131,129,194,192,195,193,2,0,3,1,66,64,67,65},{134,132,135,133,..., dimensions={0} | all-to-all | bytes 2752512 | tf_op jit(solution)/shard_map/all_to_all | solution.py:293
  43.5 0.2 convert_reduce_fusion
  43.8 13.9 %all_to_all.21.pieces = f32[8,42,128]{2,1,0:T(8,128)S(1)} all-to-all(f32[8,42,128]{2,1,0:T(8,128)S(1)} %bitcast.13), channel_id=1, replica_groups={{16,20,24,28,0,4,8,12},{17,21,25,29,1,5,9,13},{18,22,26,30,2,6,10,14},{..., dimensions={0} | all-to-all | bytes 344064 | tf_op jit(solution)/shard_map/all_to_all | solution.py:293
  57.7 0.1 merged.1
  57.8 10.2 %all_to_all.22.gathered = bf16[8,42,128]{2,1,0:T(8,128)(2,1)S(1)} all-to-all(bf16[8,42,128]{2,1,0:T(8,128)(2,1)S(1)} %get-tuple-element.12), channel_id=1, replica_groups={{128,160,192,224,0,32,64,96},{129,161,193,225,1,33,65,97},{130,162,194,..., dimensions={0} | all-to-all | bytes 172032 | tf_op jit(solution)/shard_map/all_to_all | solution.py:293
  68.0 0.3 gram_part.1
  68.3 16.1 %all_to_all.23 = bf16[32,4,1024]{2,1,0:T(4,128)(2,1)S(1)} all-to-all(bf16[32,4,1024]{2,1,0:T(4,128)(2,1)S(1)} %gram_part.1), channel_id=1, replica_groups={{18,16,19,17,22,20,23,21,26,24,27,25,30,28,31,29,2,0,3,1,6,4,7,5,10,8,1..., dimensions={0} | all-to-all | bytes 524288 | tf_op jit(solution)/shard_map/all_to_all | solution.py:293
  84.4 0.7 convert_reduce_fusion.1
  (1 shorter events, 0.0 us)
Async XLA Ops:
  13.9 6.1 %collective-permute-start = (bf16[4,4,2,168,128]{4,3,2,1,0:T(8,128)(2,1)S(1)}, bf16[4,4,2,168,128]{4,3,2,1,0:T(8,128)(2,1)S(1)}, u32[]{:S(2)}, u32[]{:S(2)}) collective-permute-start(bf16[4,4,2,168,128]{4,3,2,1,0:T(8,128)(2,1)S(1)} %get-tuple-element.10), channel_id=1, source_target_pairs={{0,32},{32,0},{1,33},{33,1},{2,34},{34,2},{3,35},{35,3},{4,36},{36... | collective-permute-start | bytes 4128776 | tf_op jit(solution)/shard_map/ppermute | solution.py:301

commit v5 on v4

v5 whole, which is shorter than its diff:
```python
import jax
import jax.numpy as jnp
from jax import lax
from jax.experimental import pallas as pl
from jax.experimental.pallas import tpu as pltpu
from jax.sharding import Mesh
from jax.sharding import PartitionSpec as P

NB = 16
R = 48
BS = 64
HALF = BS // 2
QUARTER = BS // 4
PAIRS = R // 2
BLK = 8
QB = R // BLK
TRI = QB * (QB + 1) // 2
ROWS = TRI * BLK
LANES = 2 * BS
STRIDE = 105
F32 = jnp.float32
BF16 = jnp.bfloat16

ORDER_Y = (2, 3, 0, 1)
ORDER_X = (2, 0, 3, 1)
ORDER_Z = (4, 5, 6, 7, 2, 3, 0, 1)
ORDER_YC = (4, 5, 6, 7, 2, 3, 0, 1)
ORDER_ZX = tuple(4 * z + x for z in (4, 5, 6, 7, 0, 1, 2, 3) for x in ORDER_X)

NN = (((1,), (0,)), ((), ()))
NT = (((1,), (1,)), ((), ()))
TN = (((0,), (0,)), ((), ()))


def dot(a, b, dims=NN):
    return lax.dot_general(a, b, dims, preferred_element_type=F32)


def local_kernel(
    own, core, blocks, basis_hbm, acc, send,
    stored, basis, arrived, bases, masked, swapped, wide, wide1, wide0, wide2, with_y, with_x,
):
    slots = blocks.shape[0]

    def low(rows):
        return lax.broadcasted_iota(jnp.int32, (rows, LANES), 1) < BS

    def tile(i):
        return slice(i * LANES, (i + 1) * LANES)

    def paired(first, second):
        mask = low(first.shape[0])
        return (
            jnp.where(mask, first, pltpu.roll(second, BS, 1)),
            jnp.where(mask, pltpu.roll(first, BS, 1), second),
        )

    def row_of_each(ref, row, count=HALF):
        return ref[pl.ds(row, count, stride=STRIDE), :]

    def fetch(slot):
        return pltpu.make_async_copy(blocks.at[slot], stored.at[slot], arrived.at[slot])

    fetch_basis = pltpu.make_async_copy(basis_hbm, basis, arrived.at[slots])
    fetch_basis.start()
    for slot in range(slots):
        fetch(slot).start()
    acc[...] = jnp.zeros_like(acc)
    fetch_basis.wait()
    for j in range(NB // 2):
        columns = basis[:, tile(j)]
        bases[2 * j] = columns[:, :BS]
        bases[2 * j + 1] = columns[:, BS:]

    def each_slot(slot, carry):
        fetch(slot).wait()
        one_slot(slot)
        return carry

    def one_slot(slot):
        v0 = own[0, slot]
        v1 = own[1, slot]
        v2 = own[2, slot]

        @pl.when(v0 >= 0)
        def _():
            u0 = bases[v0]
            u1 = bases[v1]
            u2 = bases[v2]
            zero = jnp.zeros_like(u0)

            def twice(u):
                return jnp.concatenate(
                    [jnp.concatenate([u, zero], 1), jnp.concatenate([zero, u], 1)], 0
                )

            both0 = twice(u0)
            both2 = twice(u2)
            both02 = jnp.concatenate([both0, both2], 1)

            for c in range(HALF // 2):
                first = stored[slot, :, tile(c)].astype(F32)
                second = stored[slot, :, tile(c + HALF // 2)].astype(F32)
                for k, part in enumerate(paired(first, second)):
                    i = 2 * c + k
                    wide[i * STRIDE : i * STRIDE + BS, :] = part
                    masked[:, tile(i)] = part.astype(BF16)

            front = v0 == v1
            back = v1 == v2

            @pl.when(front | back)
            def _():
                x = lax.broadcasted_iota(jnp.int32, (BS, LANES), 0)
                lane = lax.broadcasted_iota(jnp.int32, (BS, LANES), 1)
                z = lane & (BS - 1)
                y_high = jnp.where(lane < BS, 0, HALF)
                order_xy = jnp.where(front, (y_high - x).astype(F32) * 0.5 + 0.5, 2.0 * BS)
                order_yz = jnp.where(back, (z - y_high).astype(F32) * 0.5 + 0.5, 2.0 * BS)

                def scale(i, carry):
                    step = i.astype(F32) * 0.5
                    w = jnp.clip(order_xy + step, 0.0, 1.0) * jnp.clip(order_yz - step, 0.0, 1.0)
                    w = jnp.where(w == 0.25, 1.0 / 6.0, w)
                    rows = pl.ds(i * STRIDE, BS)
                    scaled = wide[rows, :] * w
                    wide[rows, :] = scaled
                    masked[:, pl.ds(pl.multiple_of(i * LANES, LANES), LANES)] = scaled.astype(BF16)
                    return carry

                lax.fori_loop(0, HALF, scale, 0, unroll=4)

            for i in range(HALF):
                upper, lower = paired(row_of_each(wide, i), row_of_each(wide, i + HALF))
                swapped[:HALF, tile(i)] = upper.astype(BF16)
                swapped[HALF:, tile(i)] = lower.astype(BF16)

            def spread(values, ref, target, place):
                for i in range(HALF):
                    ref[i * STRIDE : i * STRIDE + R, :] = values[:, tile(i)]
                for j in range(PAIRS):
                    upper, lower = paired(row_of_each(ref, 2 * j), row_of_each(ref, 2 * j + 1))
                    target[:HALF, tile(place(j))] = upper.astype(BF16)
                    target[HALF:, tile(place(j))] = lower.astype(BF16)

            spread(dot(u1, swapped[...]), wide1, with_x, lambda j: j)
            spread(dot(u0, masked[...]), wide0, with_y, lambda j: 2 * j + 1)
            for i in range(QUARTER):
                both_tiles = [masked[:, tile(i)], masked[:, tile(i + QUARTER)]]
                wide2[i * STRIDE : i * STRIDE + 2 * R, :] = dot(
                    both2, jnp.concatenate(both_tiles, 0), NT
                )
            for j in range(PAIRS):
                for k in range(2):
                    parts = paired(
                        row_of_each(wide2, k * R + 2 * j, QUARTER),
                        row_of_each(wide2, k * R + 2 * j + 1, QUARTER),
                    )
                    for h in range(2):
                        top = (2 * k + h) * QUARTER
                        with_y[top : top + QUARTER, tile(2 * j)] = parts[h].astype(BF16)

            def place(v):
                group = sum(jnp.where(v // 4 == y, i, 0) for i, y in enumerate(ORDER_Y))
                return ((v // 2) % 2) ^ core[0], group, v % 2

            places = [place(v) for v in (v0, v1, v2)]

            def add(f, j, value):
                side, group, half = places[f]
                block = (side, group, j % 4, half)
                q = j // 4
                start = BLK * (q * (q + 1) // 2)
                rows = BLK * (q + 1)
                at = (*block, slice(start, start + rows), slice(None))
                acc[at] = acc[at] + value[:rows]

            def stacked(ref, tiles):
                return jnp.concatenate([ref[:, t] for t in tiles], 0)

            for g in range(QB // 2):
                rows = 2 * BLK * (g + 1)
                tiles = range(8 * g, 8 * g + 8)
                span_y = slice(16 * g * LANES, 16 * (g + 1) * LANES)
                span_x = slice(8 * g * LANES, 8 * (g + 1) * LANES)
                over_y = dot(u1[:rows], with_y[:, span_y])
                over_x = dot(u0[:rows], with_x[:, span_x])
                kept2 = jnp.concatenate([both2[:rows], both2[R : R + rows]], 0)
                kept02 = jnp.concatenate([both02[:rows], both02[R : R + rows]], 0)
                lanes_x = dot(kept2, stacked(with_x, [tile(j) for j in tiles]), NT)
                lanes_y = dot(
                    kept02,
                    stacked(with_y, [slice(2 * j * LANES, (2 * j + 2) * LANES) for j in tiles]),
                    NT,
                )
                for k in range(4):
                    from_x = paired(lanes_x[:rows, tile(k)], lanes_x[rows:, tile(k)])
                    from_y = paired(lanes_y[:rows, tile(k)], lanes_y[rows:, tile(k)])
                    for h in range(2):
                        i = 2 * k + h
                        j = 8 * g + i
                        add(0, j, over_y[:, tile(2 * i)] + from_x[h])
                        add(1, j, from_y[h])
                        add(2, j, over_y[:, tile(2 * i + 1)] + over_x[:, tile(i)])

    lax.fori_loop(0, slots, each_slot, 0)

    def write(m, carry):
        send[m] = acc[1, m].astype(BF16)
        return carry

    lax.fori_loop(0, 4, write, 0)


def in_hbm(array):
    return pltpu.with_memory_space_constraint(array, pltpu.HBM)


def local_products(blocks, ownership, basis, core):
    slots = blocks.shape[0]
    half = (4, 4, 2, ROWS, LANES)
    in_vmem = pl.BlockSpec(memory_space=pltpu.VMEM)
    in_smem = pl.BlockSpec(memory_space=pltpu.SMEM)
    outside = pl.BlockSpec(memory_space=pltpu.HBM)
    return pl.pallas_call(
        local_kernel,
        in_specs=[in_smem, in_smem, outside, outside],
        out_specs=[in_vmem, in_vmem],
        scratch_shapes=[
            pltpu.VMEM(blocks.shape, BF16),
            pltpu.VMEM(basis.shape, BF16),
            pltpu.SemaphoreType.DMA((slots + 1,)),
            pltpu.VMEM((NB, R, BS), BF16),
            pltpu.VMEM((BS, BS * BS), BF16),
            pltpu.VMEM((BS, BS * BS), BF16),
            pltpu.VMEM((HALF * STRIDE, LANES), F32),
            pltpu.VMEM((HALF * STRIDE, LANES), F32),
            pltpu.VMEM((HALF * STRIDE, LANES), F32),
            pltpu.VMEM((QUARTER * STRIDE, LANES), F32),
            pltpu.VMEM((BS, 2 * PAIRS * LANES), BF16),
            pltpu.VMEM((BS, PAIRS * LANES), BF16),
        ],
        out_shape=[
            jax.ShapeDtypeStruct((2, *half), F32),
            jax.ShapeDtypeStruct(half, BF16),
        ],
        compiler_params=pltpu.CompilerParams(vmem_limit_bytes=36 << 20),
        name="local_products",
    )(in_hbm(ownership.T), core, in_hbm(blocks), in_hbm(basis))


def gram_kernel(mine, gathered, out):
    pair = lax.broadcasted_iota(jnp.int32, mine.shape, 0)
    pair = jnp.where(pair < TRI, pair, pair - TRI)
    on_diagonal = pair < 0
    for q in range(QB):
        on_diagonal = on_diagonal | (pair == q * (q + 3) // 2)
    weighted = (mine[...].astype(F32) * jnp.where(on_diagonal, 1.0, 2.0)).astype(BF16)
    everyone = jnp.concatenate([gathered[ORDER_YC.index(g)] for g in range(len(ORDER_YC))], 1)
    gram = dot(weighted, everyone, TN) / R
    for i, place in enumerate(ORDER_ZX):
        out[i] = gram[4 * place : 4 * place + 4].astype(out.dtype)


def gram_part(mine, gathered):
    return pl.pallas_call(
        gram_kernel,
        in_specs=[pl.BlockSpec(memory_space=pltpu.VMEM)] * 2,
        out_specs=pl.BlockSpec(memory_space=pltpu.VMEM),
        out_shape=jax.ShapeDtypeStruct((32, 4, NB * BS), BF16),
        compiler_params=pltpu.CompilerParams(vmem_limit_bytes=16 << 20),
        name="gram_part",
    )(mine, gathered)


def merge_kernel(pieces, out, copies):
    total = pieces[0]
    for i in range(1, pieces.shape[0]):
        total = total + pieces[i]
    low = lax.broadcasted_iota(jnp.int32, (TRI, LANES), 1) < BS
    first = total[:TRI]
    second = total[TRI:]
    upper = jnp.where(low, first, pltpu.roll(second, BS, 1)).astype(BF16)
    lower = jnp.where(low, pltpu.roll(first, BS, 1), second).astype(BF16)
    for ref in (out, *(copies.at[g] for g in range(copies.shape[0]))):
        ref[:TRI] = upper
        ref[TRI:] = lower


def merged(pieces):
    return pl.pallas_call(
        merge_kernel,
        in_specs=[pl.BlockSpec(memory_space=pltpu.VMEM)],
        out_specs=[pl.BlockSpec(memory_space=pltpu.VMEM)] * 2,
        out_shape=[
            jax.ShapeDtypeStruct((2 * TRI, LANES), BF16),
            jax.ShapeDtypeStruct((8, 2 * TRI, LANES), BF16),
        ],
        compiler_params=pltpu.CompilerParams(vmem_limit_bytes=16 << 20),
        name="merged",
    )(pieces)


def exchange(pieces, axes, order):
    return lax.all_to_all(
        pieces, axes, 0, 0, axis_index_groups=[list(order)], tiled=True
    )


def local(blocks, ownership, basis_rows):
    core = lax.axis_index("gx_1").astype(jnp.int32).reshape(1)
    kept, sent = local_products(blocks, ownership, basis_rows.T, core)
    arrived = lax.ppermute(sent, "gx_1", [(0, 1), (1, 0)])
    pair = (kept[0] + arrived.astype(F32)).astype(BF16)
    ranks = [4 * y + x for y in ORDER_Y for x in ORDER_X]
    pieces = exchange(pair.reshape(16, 2 * ROWS, LANES), ("gx_0", "gz"), ranks)
    plane = pieces.astype(F32).sum(axis=0)
    plane = plane.reshape(2 * TRI, BLK, LANES).swapaxes(0, 1)
    rounded, copies = merged(exchange(plane, "gy", ORDER_Z))
    gathered = exchange(copies, ("gx_0", "gx_1"), ORDER_YC)
    pieces = exchange(gram_part(rounded, gathered), ("gy", "gz"), ORDER_ZX)
    return pieces.astype(F32).sum(axis=0)


def solution(mesh):
    axes = ("gx_0", "gx_1", "gy", "gz")
    split = Mesh(mesh.devices.reshape(4, 2, mesh.shape["gy"], mesh.shape["gz"]), axes)
    return jax.shard_map(
        local,
        mesh=split,
        in_specs=(P(axes, None, None), P(axes, None), P()),
        out_specs=P(axes, None),
        check_vma=False,
    )
```

time: 85.2 us -> 84.7 us (level)
  starting transfers between devices: 3.3 us -> 0.09 us
  blocking collectives: 63.5 us -> 65.8 us
    ppermute x1, starting transfers between devices: 3.3 us -> 0.09 us  [local(): arrived = lax.ppermute(sent, 'gx_1', [(0, 1), (1, 0)])]
    all_to_all x4, blocking collectives: 63.5 us -> 65.8 us  [exchange(): lax.all_to_all(pieces, axes, 0, 0, axis_index_groups=[list(order)], tiled...]
where the time goes in v5:
time: 84.7 us; the launch traced here: 84.4 us
  blocking collectives  65.8 us (78%)
  Pallas kernels  14.2 us (17%)
  waiting for transfers between devices  3.12 us (4%)
  other arithmetic  1.19 us (1%)
    all_to_all x4, blocking collectives, exchange(): lax.all_to_all(pieces, axes, 0, 0, axis_index_groups=[list(order)], tiled...  65.8 us
    pallas_call x1, Pallas kernels, local_products(): pl.pallas_call(local_kernel, in_specs=[in_smem, in_smem, outside, outside...  13.8 us
    ppermute x1, waiting for transfers between devices, local(): arrived = lax.ppermute(sent, 'gx_1', [(0, 1), (1, 0)])  3.12 us
  transfers between devices with their start and end apart: 1, of which 1 were waited for; matrix products, arithmetic and copies ran while one was open for 0% of the time, Pallas kernels for 0%

profile of v5, /device:TPU:1, one launch (start us, length us, event | category | flops | bytes accessed | tf_op | source)
XLA Modules:
  0.0 84.4 jit_solution(11246341200598406379)
XLA Ops:
  0.0 13.8 %local_products.1 = (f32[2,4,4,2,168,128]{5,4,3,2,1,0:T(8,128)S(1)}, bf16[4,4,2,168,128]{4,3,2,1,0:T(8,128)(2,1)S(1)}) custom-call(s32[3,6]{1,0:T(4,128)} %bitcast.16, s32[1]{0:T(128)} %bitcast.1.core, bf16[6,64,4096]{2,1,0:T(8,128)(2,1)} %blocks.1, bf16[48,1024]{1,0:T(8,128)(2,1)} %bitcast.15), custom_call_target="tpu_custom_call" | custom-call | tf_op jit(solution)/shard_map/local_products/pallas_call | solution.py:225
  13.8 0.1 collective-permute-start
  13.9 3.1 %collective-permute-done = bf16[4,4,2,168,128]{4,3,2,1,0:T(8,128)(2,1)S(1)} collective-permute-done((bf16[4,4,2,168,128]{4,3,2,1,0:T(8,128)(2,1)S(1)}, bf16[4,4,2,168,128]{4,3,2,1,0:T(8,128)(2,1)S(1)}, u32[]{:S(2)}, u32[]{:S(2)}) %collective-permute-start) | collective-permute-done | bytes 1376288 | tf_op jit(solution)/shard_map/ppermute | solution.py:313
  17.0 0.3 fusion
  17.3 26.0 %all_to_all.20 = bf16[16,336,128]{2,1,0:T(8,128)(2,1)S(1)} all-to-all(bf16[16,336,128]{2,1,0:T(8,128)(2,1)S(1)} %bitcast.12), channel_id=1, replica_groups={{130,128,131,129,194,192,195,193,2,0,3,1,66,64,67,65},{134,132,135,133,..., dimensions={0} | all-to-all | bytes 2752512 | tf_op jit(solution)/shard_map/all_to_all | solution.py:305
  43.3 0.2 convert_reduce_fusion
  43.6 14.0 %all_to_all.21.pieces = f32[8,42,128]{2,1,0:T(8,128)S(1)} all-to-all(f32[8,42,128]{2,1,0:T(8,128)S(1)} %bitcast.13), channel_id=1, replica_groups={{16,20,24,28,8,12,0,4},{17,21,25,29,9,13,1,5},{18,22,26,30,10,14,2,6},{..., dimensions={0} | all-to-all | bytes 344064 | tf_op jit(solution)/shard_map/all_to_all | solution.py:305
  57.5 0.1 merged.1
  57.6 9.5 %all_to_all.22.gathered = bf16[8,42,128]{2,1,0:T(8,128)(2,1)S(1)} all-to-all(bf16[8,42,128]{2,1,0:T(8,128)(2,1)S(1)} %get-tuple-element.12), channel_id=1, replica_groups={{128,160,192,224,64,96,0,32},{129,161,193,225,65,97,1,33},{130,162,194,..., dimensions={0} | all-to-all | bytes 172032 | tf_op jit(solution)/shard_map/all_to_all | solution.py:305
  67.1 0.3 gram_part.1
  67.4 16.3 %all_to_all.23 = bf16[32,4,1024]{2,1,0:T(4,128)(2,1)S(1)} all-to-all(bf16[32,4,1024]{2,1,0:T(4,128)(2,1)S(1)} %gram_part.1), channel_id=1, replica_groups={{18,16,19,17,22,20,23,21,26,24,27,25,30,28,31,29,2,0,3,1,6,4,7,5,10,8,1..., dimensions={0} | all-to-all | bytes 524288 | tf_op jit(solution)/shard_map/all_to_all | solution.py:305
  83.7 0.7 convert_reduce_fusion.1
  (1 shorter events, 0.0 us)
Async XLA Ops:
  13.8 3.2 %collective-permute-start = (bf16[4,4,2,168,128]{4,3,2,1,0:T(8,128)(2,1)S(1)}, bf16[4,4,2,168,128]{4,3,2,1,0:T(8,128)(2,1)S(1)}, u32[]{:S(2)}, u32[]{:S(2)}) collective-permute-start(bf16[4,4,2,168,128]{4,3,2,1,0:T(8,128)(2,1)S(1)} %get-tuple-element.10), channel_id=1, source_target_pairs={{0,32},{32,0},{1,33},{33,1},{2,34},{34,2},{3,35},{35,3},{4,36},{36... | collective-permute-start | bytes 4128776 | tf_op jit(solution)/shard_map/ppermute | solution.py:313

commit v6 on v5

--- a/solution.py
+++ b/solution.py
@@ -18,6 +18,7 @@
 ROWS = TRI * BLK
 LANES = 2 * BS
 STRIDE = 105
+CHUNK = 4
 F32 = jnp.float32
 BF16 = jnp.bfloat16
 
@@ -135,16 +136,19 @@
                 swapped[:HALF, tile(i)] = upper.astype(BF16)
                 swapped[HALF:, tile(i)] = lower.astype(BF16)
 
-            def spread(values, ref, target, place):
-                for i in range(HALF):
-                    ref[i * STRIDE : i * STRIDE + R, :] = values[:, tile(i)]
+            def spread(factor, source, ref, target, place):
+                for c in range(0, HALF, CHUNK):
+                    values = dot(factor, source[:, c * LANES : (c + CHUNK) * LANES])
+                    for k in range(CHUNK):
+                        start = (c + k) * STRIDE
+                        ref[start : start + R, :] = values[:, tile(k)]
                 for j in range(PAIRS):
                     upper, lower = paired(row_of_each(ref, 2 * j), row_of_each(ref, 2 * j + 1))
                     target[:HALF, tile(place(j))] = upper.astype(BF16)
                     target[HALF:, tile(place(j))] = lower.astype(BF16)
 
-            spread(dot(u1, swapped[...]), wide1, with_x, lambda j: j)
-            spread(dot(u0, masked[...]), wide0, with_y, lambda j: 2 * j + 1)
+            spread(u1, swapped, wide1, with_x, lambda j: j)
+            spread(u0, masked, wide0, with_y, lambda j: 2 * j + 1)
             for i in range(QUARTER):
                 both_tiles = [masked[:, tile(i)], masked[:, tile(i + QUARTER)]]
                 wide2[i * STRIDE : i * STRIDE + 2 * R, :] = dot(
@@ -178,11 +182,12 @@
             def stacked(ref, tiles):
                 return jnp.concatenate([ref[:, t] for t in tiles], 0)
 
-            for g in range(QB // 2):
+            for q in range(QB):
+                g = q // 2
                 rows = 2 * BLK * (g + 1)
-                tiles = range(8 * g, 8 * g + 8)
-                span_y = slice(16 * g * LANES, 16 * (g + 1) * LANES)
-                span_x = slice(8 * g * LANES, 8 * (g + 1) * LANES)
+                tiles = range(4 * q, 4 * q + 4)
+                span_y = slice(8 * q * LANES, 8 * (q + 1) * LANES)
+                span_x = slice(4 * q * LANES, 4 * (q + 1) * LANES)
                 over_y = dot(u1[:rows], with_y[:, span_y])
                 over_x = dot(u0[:rows], with_x[:, span_x])
                 kept2 = jnp.concatenate([both2[:rows], both2[R : R + rows]], 0)
@@ -193,12 +198,12 @@
                     stacked(with_y, [slice(2 * j * LANES, (2 * j + 2) * LANES) for j in tiles]),
                     NT,
                 )
-                for k in range(4):
+                for k in range(2):
                     from_x = paired(lanes_x[:rows, tile(k)], lanes_x[rows:, tile(k)])
                     from_y = paired(lanes_y[:rows, tile(k)], lanes_y[rows:, tile(k)])
                     for h in range(2):
                         i = 2 * k + h
-                        j = 8 * g + i
+                        j = 4 * q + i
                         add(0, j, over_y[:, tile(2 * i)] + from_x[h])
                         add(1, j, from_y[h])
                         add(2, j, over_y[:, tile(2 * i + 1)] + over_x[:, tile(i)])

time: 84.7 us -> 84.5 us (level)
  starting transfers between devices: 0.09 us -> 12.2 us
  Pallas kernels: 14.2 us -> 4.59 us
  blocking collectives: 65.8 us -> 63.3 us
    ppermute x1, starting transfers between devices: 0.09 us -> 12.2 us  [local(): arrived = lax.ppermute(sent, 'gx_1', [(0, 1), (1, 0)])]
    pallas_call x1, Pallas kernels: 13.8 us -> 4.23 us  [local_products(): pl.pallas_call(local_kernel, in_specs=[in_smem, in_smem, outside, outside...]
    all_to_all x4, blocking collectives: 65.8 us -> 63.3 us  [exchange(): lax.all_to_all(pieces, axes, 0, 0, axis_index_groups=[list(order)], tiled...]
where the time goes in v6:
time: 84.5 us; the launch traced here: 84.2 us
  blocking collectives  63.3 us (75%)
  starting transfers between devices  12.2 us (14%)
  Pallas kernels  4.59 us (5%)
  waiting for transfers between devices  2.76 us (3%)
  other arithmetic  1.19 us (1%)
    all_to_all x4, blocking collectives, exchange(): lax.all_to_all(pieces, axes, 0, 0, axis_index_groups=[list(order)], tiled...  63.3 us
    ppermute x1, starting transfers between devices, local(): arrived = lax.ppermute(sent, 'gx_1', [(0, 1), (1, 0)])  12.2 us
    pallas_call x1, Pallas kernels, local_products(): pl.pallas_call(local_kernel, in_specs=[in_smem, in_smem, outside, outside...  4.23 us
    ppermute x1, waiting for transfers between devices, local(): arrived = lax.ppermute(sent, 'gx_1', [(0, 1), (1, 0)])  2.76 us
  transfers between devices with their start and end apart: 1, of which 1 were waited for; matrix products, arithmetic and copies ran while one was open for 0% of the time, Pallas kernels for 0%

profile of v6, /device:TPU:1, one launch (start us, length us, event | category | flops | bytes accessed | tf_op | source)
XLA Modules:
  0.0 84.2 jit_solution(14665409841463939887)
XLA Ops:
  0.0 4.2 %local_products.1 = (f32[2,4,4,2,168,128]{5,4,3,2,1,0:T(8,128)S(1)}, bf16[4,4,2,168,128]{4,3,2,1,0:T(8,128)(2,1)S(1)}) custom-call(s32[3,6]{1,0:T(4,128)} %bitcast.16, s32[1]{0:T(128)} %bitcast.1.core, bf16[6,64,4096]{2,1,0:T(8,128)(2,1)} %blocks.1, bf16[48,1024]{1,0:T(8,128)(2,1)} %bitcast.15), custom_call_target="tpu_custom_call" | custom-call | tf_op jit(solution)/shard_map/local_products/pallas_call | solution.py:230
  4.2 12.2 %collective-permute-start = (bf16[4,4,2,168,128]{4,3,2,1,0:T(8,128)(2,1)S(1)}, bf16[4,4,2,168,128]{4,3,2,1,0:T(8,128)(2,1)S(1)}, u32[]{:S(2)}, u32[]{:S(2)}) collective-permute-start(bf16[4,4,2,168,128]{4,3,2,1,0:T(8,128)(2,1)S(1)} %get-tuple-element.10), channel_id=1, source_target_pairs={{0,32},{32,0},{1,33},{33,1},{2,34},{34,2},{3,35},{35,3},{4,36},{36... | collective-permute-start | bytes 4128776 | tf_op jit(solution)/shard_map/ppermute | solution.py:318
  16.5 2.8 %collective-permute-done = bf16[4,4,2,168,128]{4,3,2,1,0:T(8,128)(2,1)S(1)} collective-permute-done((bf16[4,4,2,168,128]{4,3,2,1,0:T(8,128)(2,1)S(1)}, bf16[4,4,2,168,128]{4,3,2,1,0:T(8,128)(2,1)S(1)}, u32[]{:S(2)}, u32[]{:S(2)}) %collective-permute-start) | collective-permute-done | bytes 1376288 | tf_op jit(solution)/shard_map/ppermute | solution.py:318
  19.2 0.3 fusion
  19.5 24.1 %all_to_all.20 = bf16[16,336,128]{2,1,0:T(8,128)(2,1)S(1)} all-to-all(bf16[16,336,128]{2,1,0:T(8,128)(2,1)S(1)} %bitcast.12), channel_id=1, replica_groups={{130,128,131,129,194,192,195,193,2,0,3,1,66,64,67,65},{134,132,135,133,..., dimensions={0} | all-to-all | bytes 2752512 | tf_op jit(solution)/shard_map/all_to_all | solution.py:310
  43.6 0.2 convert_reduce_fusion
  43.8 12.9 %all_to_all.21.pieces = f32[8,42,128]{2,1,0:T(8,128)S(1)} all-to-all(f32[8,42,128]{2,1,0:T(8,128)S(1)} %bitcast.13), channel_id=1, replica_groups={{16,20,24,28,8,12,0,4},{17,21,25,29,9,13,1,5},{18,22,26,30,10,14,2,6},{..., dimensions={0} | all-to-all | bytes 344064 | tf_op jit(solution)/shard_map/all_to_all | solution.py:310
  56.8 0.1 merged.1
  56.9 10.0 %all_to_all.22.gathered = bf16[8,42,128]{2,1,0:T(8,128)(2,1)S(1)} all-to-all(bf16[8,42,128]{2,1,0:T(8,128)(2,1)S(1)} %get-tuple-element.12), channel_id=1, replica_groups={{128,160,192,224,64,96,0,32},{129,161,193,225,65,97,1,33},{130,162,194,..., dimensions={0} | all-to-all | bytes 172032 | tf_op jit(solution)/shard_map/all_to_all | solution.py:310
  66.8 0.3 gram_part.1
  67.1 16.3 %all_to_all.23 = bf16[32,4,1024]{2,1,0:T(4,128)(2,1)S(1)} all-to-all(bf16[32,4,1024]{2,1,0:T(4,128)(2,1)S(1)} %gram_part.1), channel_id=1, replica_groups={{18,16,19,17,22,20,23,21,26,24,27,25,30,28,31,29,2,0,3,1,6,4,7,5,10,8,1..., dimensions={0} | all-to-all | bytes 524288 | tf_op jit(solution)/shard_map/all_to_all | solution.py:310
  83.4 0.7 convert_reduce_fusion.1
  (1 shorter events, 0.0 us)
Async XLA Ops:
  4.2 15.0 %collective-permute-start = (bf16[4,4,2,168,128]{4,3,2,1,0:T(8,128)(2,1)S(1)}, bf16[4,4,2,168,128]{4,3,2,1,0:T(8,128)(2,1)S(1)}, u32[]{:S(2)}, u32[]{:S(2)}) collective-permute-start(bf16[4,4,2,168,128]{4,3,2,1,0:T(8,128)(2,1)S(1)} %get-tuple-element.10), channel_id=1, source_target_pairs={{0,32},{32,0},{1,33},{33,1},{2,34},{34,2},{3,35},{35,3},{4,36},{36... | collective-permute-start | bytes 4128776 | tf_op jit(solution)/shard_map/ppermute | solution.py:318

commit v7 on v6

--- a/solution.py
+++ b/solution.py
@@ -238,10 +238,10 @@
             pltpu.VMEM((NB, R, BS), BF16),
             pltpu.VMEM((BS, BS * BS), BF16),
             pltpu.VMEM((BS, BS * BS), BF16),
-            pltpu.VMEM((HALF * STRIDE, LANES), F32),
-            pltpu.VMEM((HALF * STRIDE, LANES), F32),
-            pltpu.VMEM((HALF * STRIDE, LANES), F32),
-            pltpu.VMEM((QUARTER * STRIDE, LANES), F32),
+            pltpu.VMEM((HALF * STRIDE + 112, LANES), F32),
+            pltpu.VMEM((HALF * STRIDE + 112, LANES), F32),
+            pltpu.VMEM((HALF * STRIDE + 112, LANES), F32),
+            pltpu.VMEM((QUARTER * STRIDE + 112, LANES), F32),
             pltpu.VMEM((BS, 2 * PAIRS * LANES), BF16),
             pltpu.VMEM((BS, PAIRS * LANES), BF16),
         ],

time: 84.5 us -> 83.8 us (level)
  Pallas kernels: 4.59 us -> 13.5 us
  starting transfers between devices: 12.2 us -> 3.6 us
  blocking collectives: 63.3 us -> 62.4 us
    pallas_call x1, Pallas kernels: 4.23 us -> 13.2 us  [local_products(): pl.pallas_call(local_kernel, in_specs=[in_smem, in_smem, outside, outside...]
    ppermute x1, starting transfers between devices: 12.2 us -> 3.6 us  [local(): arrived = lax.ppermute(sent, 'gx_1', [(0, 1), (1, 0)])]
    all_to_all x4, blocking collectives: 63.3 us -> 62.4 us  [exchange(): lax.all_to_all(pieces, axes, 0, 0, axis_index_groups=[list(order)], tiled...]
where the time goes in v7:
time: 83.8 us; the launch traced here: 83.5 us
  blocking collectives  62.4 us (74%)
  Pallas kernels  13.5 us (16%)
  starting transfers between devices  3.6 us (4%)
  waiting for transfers between devices  2.76 us (3%)
  other arithmetic  1.19 us (1%)
    all_to_all x4, blocking collectives, exchange(): lax.all_to_all(pieces, axes, 0, 0, axis_index_groups=[list(order)], tiled...  62.4 us
    pallas_call x1, Pallas kernels, local_products(): pl.pallas_call(local_kernel, in_specs=[in_smem, in_smem, outside, outside...  13.2 us
    ppermute x1, starting transfers between devices, local(): arrived = lax.ppermute(sent, 'gx_1', [(0, 1), (1, 0)])  3.6 us
    ppermute x1, waiting for transfers between devices, local(): arrived = lax.ppermute(sent, 'gx_1', [(0, 1), (1, 0)])  2.76 us
  transfers between devices with their start and end apart: 1, of which 1 were waited for; matrix products, arithmetic and copies ran while one was open for 0% of the time, Pallas kernels for 0%

profile of v7, /device:TPU:1, one launch (start us, length us, event | category | flops | bytes accessed | tf_op | source)
XLA Modules:
  0.0 83.5 jit_solution(15083436443862528129)
XLA Ops:
  0.0 13.2 %local_products.1 = (f32[2,4,4,2,168,128]{5,4,3,2,1,0:T(8,128)S(1)}, bf16[4,4,2,168,128]{4,3,2,1,0:T(8,128)(2,1)S(1)}) custom-call(s32[3,6]{1,0:T(4,128)} %bitcast.16, s32[1]{0:T(128)} %bitcast.1.core, bf16[6,64,4096]{2,1,0:T(8,128)(2,1)} %blocks.1, bf16[48,1024]{1,0:T(8,128)(2,1)} %bitcast.15), custom_call_target="tpu_custom_call" | custom-call | tf_op jit(solution)/shard_map/local_products/pallas_call | solution.py:230
  13.2 3.6 %collective-permute-start = (bf16[4,4,2,168,128]{4,3,2,1,0:T(8,128)(2,1)S(1)}, bf16[4,4,2,168,128]{4,3,2,1,0:T(8,128)(2,1)S(1)}, u32[]{:S(2)}, u32[]{:S(2)}) collective-permute-start(bf16[4,4,2,168,128]{4,3,2,1,0:T(8,128)(2,1)S(1)} %get-tuple-element.10), channel_id=1, source_target_pairs={{0,32},{32,0},{1,33},{33,1},{2,34},{34,2},{3,35},{35,3},{4,36},{36... | collective-permute-start | bytes 4128776 | tf_op jit(solution)/shard_map/ppermute | solution.py:318
  16.8 2.8 %collective-permute-done = bf16[4,4,2,168,128]{4,3,2,1,0:T(8,128)(2,1)S(1)} collective-permute-done((bf16[4,4,2,168,128]{4,3,2,1,0:T(8,128)(2,1)S(1)}, bf16[4,4,2,168,128]{4,3,2,1,0:T(8,128)(2,1)S(1)}, u32[]{:S(2)}, u32[]{:S(2)}) %collective-permute-start) | collective-permute-done | bytes 1376288 | tf_op jit(solution)/shard_map/ppermute | solution.py:318
  19.5 0.3 fusion
  19.8 22.2 %all_to_all.20 = bf16[16,336,128]{2,1,0:T(8,128)(2,1)S(1)} all-to-all(bf16[16,336,128]{2,1,0:T(8,128)(2,1)S(1)} %bitcast.12), channel_id=1, replica_groups={{130,128,131,129,194,192,195,193,2,0,3,1,66,64,67,65},{134,132,135,133,..., dimensions={0} | all-to-all | bytes 2752512 | tf_op jit(solution)/shard_map/all_to_all | solution.py:310
  42.0 0.2 convert_reduce_fusion
  42.2 13.9 %all_to_all.21.pieces = f32[8,42,128]{2,1,0:T(8,128)S(1)} all-to-all(f32[8,42,128]{2,1,0:T(8,128)S(1)} %bitcast.13), channel_id=1, replica_groups={{16,20,24,28,8,12,0,4},{17,21,25,29,9,13,1,5},{18,22,26,30,10,14,2,6},{..., dimensions={0} | all-to-all | bytes 344064 | tf_op jit(solution)/shard_map/all_to_all | solution.py:310
  56.1 0.1 merged.1
  56.2 10.0 %all_to_all.22.gathered = bf16[8,42,128]{2,1,0:T(8,128)(2,1)S(1)} all-to-all(bf16[8,42,128]{2,1,0:T(8,128)(2,1)S(1)} %get-tuple-element.12), channel_id=1, replica_groups={{128,160,192,224,64,96,0,32},{129,161,193,225,65,97,1,33},{130,162,194,..., dimensions={0} | all-to-all | bytes 172032 | tf_op jit(solution)/shard_map/all_to_all | solution.py:310
  66.2 0.3 gram_part.1
  66.4 16.3 %all_to_all.23 = bf16[32,4,1024]{2,1,0:T(4,128)(2,1)S(1)} all-to-all(bf16[32,4,1024]{2,1,0:T(4,128)(2,1)S(1)} %gram_part.1), channel_id=1, replica_groups={{18,16,19,17,22,20,23,21,26,24,27,25,30,28,31,29,2,0,3,1,6,4,7,5,10,8,1..., dimensions={0} | all-to-all | bytes 524288 | tf_op jit(solution)/shard_map/all_to_all | solution.py:310
  82.8 0.7 convert_reduce_fusion.1
  (1 shorter events, 0.0 us)
Async XLA Ops:
  13.2 6.4 %collective-permute-start = (bf16[4,4,2,168,128]{4,3,2,1,0:T(8,128)(2,1)S(1)}, bf16[4,4,2,168,128]{4,3,2,1,0:T(8,128)(2,1)S(1)}, u32[]{:S(2)}, u32[]{:S(2)}) collective-permute-start(bf16[4,4,2,168,128]{4,3,2,1,0:T(8,128)(2,1)S(1)} %get-tuple-element.10), channel_id=1, source_target_pairs={{0,32},{32,0},{1,33},{33,1},{2,34},{34,2},{3,35},{35,3},{4,36},{36... | collective-permute-start | bytes 4128776 | tf_op jit(solution)/shard_map/ppermute | solution.py:318
